TPU v7x, 768 devices: a whole 4x8x12 slice. The times are simulated.
768 devices in a mesh: lat: 16 (over y_lo, x), lon: 48 (over y_hi, z, core).
Axes of the slice: x: 4, y: 8 (y_hi: 2, y_lo: 4; y = y_hi * 4 + y_lo), z: 12, core: 2. Of those that a mesh axis runs over, the one named last changes fastest.
Arguments:
- grid_state: float32 [192, 720, 384], P('lat', 'lon'), may hold values from -6 to 6
- norm_gain: float32 [2, 384], replicated, may hold values from 0.25 to 1.75
- conv_weight: bfloat16 [2, 3, 3, 384, 384], replicated, may hold values from -0.109375 to 0.109375
- filter_weight: bfloat16 [192, 384, 384], P('lat'), may hold values from -0.3125 to 0.3125
- degree_keep: int32 [192, 192], P('lat', 'lon'), may hold values 0 or 1
Outputs:
- updated: float32 [192, 720, 384], P('lat', 'lon')
Inputs may be any that keep to these rules, and one draw needn't show every extreme that they name: degree_keep[l, m] is 0 or 1 for degree l and order m.
All inputs are finite; a program needn't handle non-finite values. No bound on the sum of `degree_keep` on one device may be relied on, other than what follows from the above.
Results may differ from a plain program's by a relative error of at most 0.008.
Values may be sent and summed in bfloat16 or wider, within the bound.
No kernel may reach another device: no remote copies, remote signals or barrier semaphores. Data moves between devices by JAX's collectives and lax.ppermute only.
A program may use at most 64 MiB of HBM per device.

v0:
```python
import math

import jax
import jax.numpy as jnp
from jax import lax
from jax.sharding import PartitionSpec as P

epsilon = 1e-06


def extended(array, sides, width):
    for axis, dim in sides:
        size, length = (lax.axis_size(axis), array.shape[dim])
        up = [(i, (i + 1) % size) for i in range(size)]
        down = [(j, i) for i, j in up]
        last = lax.slice_in_dim(array, length - width, length, axis=dim)
        first = lax.slice_in_dim(array, 0, width, axis=dim)
        before = lax.ppermute(last, axis, up)
        after = lax.ppermute(first, axis, down)
        array = jnp.concatenate([before, array, after], axis=dim)
    return array


def laid_out(pieces, dim):
    dims = list(pieces.shape[1:])
    dims[dim] *= pieces.shape[0]
    return jnp.moveaxis(pieces, 0, dim).reshape(dims)


def from_everyone(array, axis):
    length = lax.axis_size(axis)
    return lax.all_to_all(
        jnp.broadcast_to(array[None], (length, *array.shape)), axis, 0, 0, tiled=True
    )


def collect(array, axis, dim):
    return laid_out(from_everyone(array, axis), dim)


def colatitude(row_index, total_rows, float_type):
    theta_rows = (row_index.astype(float_type) + 0.5) * (math.pi / total_rows)
    return (jnp.cos(theta_rows), jnp.sin(theta_rows))


def legendre_table(orders, cosine, sine_values, amount):
    float_type = cosine.dtype
    order_f = orders.astype(float_type)[:, None]
    order_i = orders[:, None]
    column = cosine[None, :]
    log_start = (
        0.5
        * (
            jnp.log((2.0 * order_f + 1.0) / (4.0 * math.pi))
            + jax.scipy.special.gammaln(order_f + 0.5)
            - jax.scipy.special.gammaln(order_f + 1.0)
            - 0.5 * math.log(math.pi)
        )
        + order_f * jnp.log(sine_values)[None, :]
    )
    sectoral = jnp.exp(log_start)

    def advance(carry, degree):
        before, latest = carry
        degree_f = degree.astype(float_type)
        growth = jnp.sqrt(
            jnp.maximum(4.0 * degree_f * degree_f - 1.0, 1.0)
            / jnp.maximum(degree_f * degree_f - order_f * order_f, 1.0)
        )
        prior = degree_f - 1.0
        damping = jnp.sqrt(
            jnp.maximum(prior * prior - order_f * order_f, 0.0)
            / jnp.maximum(4.0 * prior * prior - 1.0, 1.0)
        )
        grown = growth * (column * latest - damping * before)
        fresh = jnp.where(
            degree < order_i, jnp.zeros_like(grown), jnp.where(degree == order_i, sectoral, grown)
        )
        return ((latest, fresh), fresh)

    zero_rows = jnp.zeros((orders.shape[0], cosine.shape[0]), float_type)
    _, assoc_basis = lax.scan(
        advance, (zero_rows, zero_rows), jnp.arange(amount, dtype=jnp.int32), unroll=16
    )
    return assoc_basis


def forward_table(columns, modes, total_cols, float_type):
    lon_index = columns[:, None]
    order_index = jnp.arange(modes, dtype=jnp.int32)[None, :]
    phase = (lon_index * order_index % total_cols).astype(float_type) * (2.0 * math.pi / total_cols)
    factor = 2.0 * math.pi / total_cols
    return jnp.stack([jnp.cos(phase) * factor, -jnp.sin(phase) * factor], axis=2).reshape(
        columns.shape[0], 2 * modes
    )


def inverse_table(modes, total_cols, float_type):
    order_index = jnp.arange(modes, dtype=jnp.int32)[:, None]
    lon_index = jnp.arange(total_cols, dtype=jnp.int32)[None, :]
    phase = (lon_index * order_index % total_cols).astype(float_type) * (2.0 * math.pi / total_cols)
    factor = jnp.where(order_index == 0, 1.0, 2.0).astype(float_type)
    return jnp.stack([jnp.cos(phase) * factor, -jnp.sin(phase) * factor], axis=1).reshape(
        2 * modes, total_cols
    )


def paired(form, data, table):
    upper_part = table.astype(jnp.bfloat16)
    lower_part = (table - upper_part.astype(jnp.float32)).astype(jnp.bfloat16)
    first = jnp.einsum(form, data, upper_part, preferred_element_type=jnp.float32)
    return first + jnp.einsum(form, data, lower_part, preferred_element_type=jnp.float32)


def to_columns(values):
    return lax.all_to_all(values, "lon", split_axis=2, concat_axis=0, tiled=True)


def to_channels(values):
    return lax.all_to_all(values, "lon", split_axis=0, concat_axis=2, tiled=True)


def grid_rims(normed):
    padded = extended(normed, (("lat", 0), ("lon", 1)), 1)
    place = lax.axis_index("lat")
    final_place = lax.axis_size("lat") - 1
    zero_line = jnp.zeros_like(padded[:1])
    upper_rim = jnp.where(place == 0, zero_line, padded[:1])
    lower_rim = jnp.where(place == final_place, zero_line, padded[-1:])
    return jnp.concatenate([upper_rim, padded[1:-1], lower_rim], axis=0)


def conv_taps(padded, weight, row_count, col_count):
    channels = padded.shape[2]
    running = jnp.zeros((row_count * col_count, weight.shape[3]), jnp.float32)
    for row_tap in range(3):
        for col_tap in range(3):
            window = padded[row_tap : row_tap + row_count, col_tap : col_tap + col_count].reshape(
                row_count * col_count, channels
            )
            running = running + jnp.dot(
                window, weight[row_tap, col_tap], preferred_element_type=jnp.float32
            )
    return running.reshape(row_count, col_count, weight.shape[3])


def conv_block(grid_state, gain, weight):
    row_count, col_count, channels = grid_state.shape
    scale_rows = lax.rsqrt(jnp.mean(grid_state * grid_state, axis=-1, keepdims=True) + epsilon)
    normed = (grid_state * scale_rows * gain).astype(jnp.bfloat16)
    padded = grid_rims(normed)
    mixture = conv_taps(padded, weight, row_count, col_count)
    return grid_state + jax.nn.gelu(mixture, approximate=False)


def per_device(grid_state, norm_gain, conv_weight, filter_weight, degree_keep):
    f32 = jnp.float32
    for depth_index in range(2):
        grid_state = conv_block(grid_state, norm_gain[depth_index], conv_weight[depth_index])
    row_count, col_count, channels = grid_state.shape
    lat_parts = lax.axis_size("lat")
    lon_parts = lax.axis_size("lon")
    total_rows = row_count * lat_parts
    total_cols = col_count * lon_parts
    local_modes = total_rows // lon_parts
    share = channels // lon_parts
    columns = to_columns(jnp.transpose(grid_state.astype(jnp.bfloat16), (1, 0, 2)))
    flat_columns = columns.reshape(total_cols, row_count * share)
    dft_table = forward_table(jnp.arange(total_cols), total_rows, total_cols, f32)
    spectrum = paired("lx,lk->kx", flat_columns, dft_table).astype(jnp.bfloat16)
    spectrum = to_channels(spectrum.reshape(2 * total_rows, row_count, share))
    spectrum = jnp.transpose(spectrum, (1, 0, 2)).reshape(row_count, local_modes, 2 * channels)
    orders = lax.axis_index("lon") * local_modes + jnp.arange(local_modes, dtype=jnp.int32)
    keep_mask = degree_keep.astype(f32)
    cosine, sine_values = colatitude(jnp.arange(total_rows), total_rows, f32)
    assoc_basis = legendre_table(orders, cosine, sine_values, total_rows)
    weighted = assoc_basis * (sine_values * (math.pi / total_rows))[None, None, :]
    first_here = lax.axis_index("lat") * row_count
    own_weighted = lax.dynamic_slice_in_dim(weighted, first_here, row_count, 0)
    own_rows_basis = lax.dynamic_slice_in_dim(assoc_basis, first_here, row_count, 2)
    basis_rows = own_weighted
    coefficients = paired("imx,lmi->lmx", collect(spectrum, "lat", 0), basis_rows).astype(
        jnp.bfloat16
    )
    flat_coeffs = coefficients.reshape(row_count, 2 * local_modes, channels)
    mixture = jnp.einsum("lkc,lcd->lkd", flat_coeffs, filter_weight, preferred_element_type=f32)
    mixture = mixture.reshape(row_count, local_modes, 2, channels) * keep_mask[:, :, None, None]
    filtered = mixture.reshape(row_count, local_modes, 2 * channels).astype(jnp.bfloat16)
    basis_rows = own_rows_basis
    synthesis = paired("lmx,lmi->imx", collect(filtered, "lat", 0), basis_rows).astype(jnp.bfloat16)
    by_order = jnp.transpose(synthesis.reshape(row_count, 2 * local_modes, channels), (1, 0, 2))
    returned = to_columns(by_order)
    flat_returned = returned.reshape(2 * total_rows, row_count * share)
    physical = paired(
        "kx,kl->lx", flat_returned, inverse_table(total_rows, total_cols, f32)
    ).astype(jnp.bfloat16)
    physical = to_channels(physical.reshape(total_cols, row_count, share))
    physical = jnp.transpose(physical, (1, 0, 2))
    return grid_state + jax.nn.gelu(physical.astype(f32), approximate=False)


def solution(mesh):
    in_specs = (P("lat", "lon", None), P(), P(), P("lat", None, None), P("lat", "lon"))
    out_specs = P("lat", "lon", None)
    return jax.shard_map(
        per_device, mesh=mesh, in_specs=in_specs, out_specs=out_specs, check_vma=False
    )
```

profile of v0, /device:TPU:1, one launch (start us, length us, event | category | flops | bytes accessed | tf_op | source)
XLA Modules:
  0.0 1031.3 jit_solution(3727784094169360064)
XLA Ops:
  3.2 3.9 collective-permute-start
  7.2 6.2 collective-permute-start.1
  16.2 5.5 collective-permute-start.2
  21.7 5.6 slice_bitcast_fusion
  29.7 8.9 collective-permute-start.3
  82.8 7.8 collective-permute-start.5
  95.3 3.4 negate_multiply_fusion
  101.0 10.8 %collective-permute-start.7 = (bf16[14,1,384]{2,0,1:T(8,128)(2,1)S(1)}, bf16[14,1,384]{2,0,1:T(8,128)(2,1)S(1)}, u32[]{:S(2)}, u32[]{:S(2)}) collective-permute-start(bf16[14,1,384]{2,0,1:T(8,128)(2,1)S(1)} %copy.351), channel_id=1, source_target_pairs={{1,0},{2,1},{3,2},{4,3},{5,4},{6,5},{7,6},{8,7},{9,8},{10,9},{11,1... | collective-permute-start | bytes 32264 | tf_op jit(solution)/shard_map/ppermute | solution.py:19
  158.4 3.7 reshape.1599
  162.1 17.3 %all-to-all-start = ((bf16[48,2,720]{2,1,0:T(2,128)(2,1)}), bf16[48,2,720]{2,1,0:T(2,128)(2,1)}, u32[]{:S(2)}, u32[]{:S(2)}) async-start(bf16[48,2,720]{2,1,0:T(2,128)(2,1)} %reshape.1599), calls=%async_computation | async-start | bytes 294912 | tf_op jit(solution)/shard_map/all_to_all | solution.py:116
  192.2 3.8 all-to-all-done
  196.0 4.6 reshape.1600
  215.4 11.6 %all-to-all-start.1 = ((bf16[48,2,384]{2,1,0:T(2,128)(2,1)}), bf16[48,2,384]{2,1,0:T(2,128)(2,1)}, u32[]{:S(2)}, u32[]{:S(2)}) async-start(bf16[48,2,384]{2,1,0:T(2,128)(2,1)} %reshape.1601), calls=%async_computation.1 | async-start | bytes 147456 | tf_op jit(solution)/shard_map/all_to_all | solution.py:120
  227.7 14.4 %all-to-all-done.1 = bf16[48,2,384]{2,1,0:T(2,128)(2,1)} async-done(((bf16[48,2,384]{2,1,0:T(2,128)(2,1)}), bf16[48,2,384]{2,1,0:T(2,128)(2,1)}, u32[]{:S(2)}, u32[]{:S(2)}) %all-to-all-start.1) | async-done | bytes 73760 | tf_op jit(solution)/shard_map/all_to_all | solution.py:120
  242.2 3.6 reshape.1602
  245.7 4.9 copy.371
  257.6 7.3 all-to-all-start.2
  265.0 607.6 %while.21 = (s32[]{:T(128)}, f32[4,192]{1,0:T(4,128)}, f32[4,192]{1,0:T(4,128)}, f32[12,16,4,192]{3,1,0,2:T(8,128)}, s32[12,16]{1,0:T(8,128)}, /*index=5*/s32[]{...) while((s32[]{:T(128)}, f32[4,192]{1,0:T(4,128)}, ...), condition=%wide.region_3.4_spmd.clone.clone.clone.clone, body=%wide.region_2.3_spmd.clone.clone.clone.clone.sunk | while | flops 102146 | bytes 500728 | solution.py:82
  885.0 6.9 all-to-all-start.3
  897.3 3.4 cosine_multiply_fusion.1
  900.7 15.6 %all-to-all-done.3 = bf16[16,12,4,768]{3,2,1,0:T(4,128)(2,1)} async-done(((bf16[16,12,4,768]{3,2,1,0:T(4,128)(2,1)}), bf16[16,12,4,768]{3,2,1,0:T(4,128)(2,1)}, u32[]{:S(2)}, u32[]{:S(2)}) %all-to-all-start.3) | async-done | bytes 1179680 | tf_op jit(solution)/shard_map/all_to_all | solution.py:32
  926.9 8.6 all-to-all-start.4
  946.4 4.3 all-to-all-done.4
  950.6 3.6 reshape.1604
  954.2 4.9 copy.383
  968.4 3.6 reshape.1605
  972.0 27.8 %all_to_all.67 = bf16[48,2,720]{2,1,0:T(2,128)(2,1)} all-to-all(bf16[48,2,720]{2,1,0:T(2,128)(2,1)} %reshape.1605), channel_id=1, replica_groups=mesh['lat'=16,'lon'=48] {'lon'}, dimensions={0} | all-to-all | bytes 276480 | tf_op jit(solution)/shard_map/all_to_all | solution.py:120
  999.8 3.3 reshape.1606
  1007.8 3.5 reshape.1590
  1011.3 3.8 copy.421
  1018.2 3.5 reshape.1593
  1021.7 3.8 copy.420
  (992 shorter events, 686.9 us)
Async XLA Ops:
  0.0 878.8 %copy-start = (bf16[12,384,384]{2,1,0:T(8,128)(2,1)S(1)}, bf16[12,384,384]{2,1,0:T(8,128)(2,1)}, u32[]{:S(2)}) copy-start(bf16[12,384,384]{2,1,0:T(8,128)(2,1)} %param.10) | copy-start | bytes 10616836
  3.2 11.0 %copy-start.4 = (bf16[12,15,384]{2,1,0:T(8,128)(2,1)}, bf16[12,15,384]{2,1,0:T(8,128)(2,1)S(1)}, u32[]{:S(2)}) copy-start(bf16[12,15,384]{2,1,0:T(8,128)(2,1)S(1)} %multiply_convert_fusion.1) | copy-start | bytes 414724
  3.2 10.2 collective-permute-start
  7.2 7.0 collective-permute-start.1
  14.2 2.0 copy-start.25
  16.2 22.4 %collective-permute-start.2 = (bf16[14,1,384]{2,0,1:T(8,128)(2,1)}, bf16[14,1,384]{2,0,1:T(8,128)(2,1)}, u32[]{:S(2)}, u32[]{:S(2)}) collective-permute-start(bf16[14,1,384]{2,0,1:T(8,128)(2,1)} %copy.418), channel_id=1, source_target_pairs={{0,1},{1,2},{2,3},{3,4},{4,5},{5,6},{6,7},{7,8},{8,9},{9,10},{10,1... | collective-permute-start | bytes 32264 | tf_op jit(solution)/shard_map/ppermute | solution.py:18
  29.7 10.6 %collective-permute-start.3 = (bf16[14,1,384]{2,0,1:T(8,128)(2,1)S(1)}, bf16[14,1,384]{2,0,1:T(8,128)(2,1)S(1)}, u32[]{:S(2)}, u32[]{:S(2)}) collective-permute-start(bf16[14,1,384]{2,0,1:T(8,128)(2,1)S(1)} %copy.419), channel_id=1, source_target_pairs={{1,0},{2,1},{3,2},{4,3},{5,4},{6,5},{7,6},{8,7},{9,8},{10,9},{11,1... | collective-permute-start | bytes 32264 | tf_op jit(solution)/shard_map/ppermute | solution.py:19
  67.2 4.1 copy-start.2
  67.2 5.3 copy-start.17
  67.2 5.6 copy-start.20
  68.6 4.4 copy-start.22
  70.0 3.4 copy-start.24
  71.3 2.3 copy-start.16
  80.0 0.7 copy-start.3
  80.8 10.6 %copy-start.5 = (bf16[12,15,384]{2,1,0:T(8,128)(2,1)}, bf16[12,15,384]{2,1,0:T(8,128)(2,1)S(1)}, u32[]{:S(2)}) copy-start(bf16[12,15,384]{2,1,0:T(8,128)(2,1)S(1)} %multiply_convert_fusion) | copy-start | bytes 414724
  80.8 9.8 collective-permute-start.4
  82.8 8.6 collective-permute-start.5
  91.4 2.0 copy-start.26
  91.5 0.7 copy-start.14
  93.4 18.4 %collective-permute-start.6 = (bf16[14,1,384]{2,0,1:T(8,128)(2,1)}, bf16[14,1,384]{2,0,1:T(8,128)(2,1)}, u32[]{:S(2)}, u32[]{:S(2)}) collective-permute-start(bf16[14,1,384]{2,0,1:T(8,128)(2,1)} %copy.350), channel_id=1, source_target_pairs={{0,1},{1,2},{2,3},{3,4},{4,5},{5,6},{6,7},{7,8},{8,9},{9,10},{10,1... | collective-permute-start | bytes 32264 | tf_op jit(solution)/shard_map/ppermute | solution.py:18
  101.0 12.5 %collective-permute-start.7 = (bf16[14,1,384]{2,0,1:T(8,128)(2,1)S(1)}, bf16[14,1,384]{2,0,1:T(8,128)(2,1)S(1)}, u32[]{:S(2)}, u32[]{:S(2)}) collective-permute-start(bf16[14,1,384]{2,0,1:T(8,128)(2,1)S(1)} %copy.351), channel_id=1, source_target_pairs={{1,0},{2,1},{3,2},{4,3},{5,4},{6,5},{7,6},{8,7},{9,8},{10,9},{11,1... | collective-permute-start | bytes 32264 | tf_op jit(solution)/shard_map/ppermute | solution.py:19
  142.1 4.1 copy-start.1
  142.1 5.3 copy-start.18
  142.1 5.6 copy-start.19
  143.6 4.4 copy-start.21
  144.9 3.4 copy-start.23
  146.2 2.3 copy-start.15
  162.1 33.8 %all-to-all-start = ((bf16[48,2,720]{2,1,0:T(2,128)(2,1)}), bf16[48,2,720]{2,1,0:T(2,128)(2,1)}, u32[]{:S(2)}, u32[]{:S(2)}) async-start(bf16[48,2,720]{2,1,0:T(2,128)(2,1)} %reshape.1599), calls=%async_computation | async-start | bytes 294912 | tf_op jit(solution)/shard_map/all_to_all | solution.py:116
  215.4 26.7 %all-to-all-start.1 = ((bf16[48,2,384]{2,1,0:T(2,128)(2,1)}), bf16[48,2,384]{2,1,0:T(2,128)(2,1)}, u32[]{:S(2)}, u32[]{:S(2)}) async-start(bf16[48,2,384]{2,1,0:T(2,128)(2,1)} %reshape.1601), calls=%async_computation.1 | async-start | bytes 147456 | tf_op jit(solution)/shard_map/all_to_all | solution.py:120
  257.6 615.8 %all-to-all-start.2 = ((bf16[16,12,4,768]{3,2,1,0:T(4,128)(2,1)}), bf16[16,12,4,768]{3,2,1,0:T(4,128)(2,1)}, u32[]{:S(2)}, u32[]{:S(2)}) async-start(bf16[16,12,4,768]{3,2,1,0:T(4,128)(2,1)} %broadcast_in_dim.483), calls=%async_computation.2 | async-start | bytes 2359296 | tf_op jit(solution)/shard_map/all_to_all | solution.py:32
  885.0 31.3 %all-to-all-start.3 = ((bf16[16,12,4,768]{3,2,1,0:T(4,128)(2,1)}), bf16[16,12,4,768]{3,2,1,0:T(4,128)(2,1)}, u32[]{:S(2)}, u32[]{:S(2)}) async-start(bf16[16,12,4,768]{3,2,1,0:T(4,128)(2,1)} %broadcast_in_dim.484), calls=%async_computation.3 | async-start | bytes 2359296 | tf_op jit(solution)/shard_map/all_to_all | solution.py:32
  926.9 23.7 %all-to-all-start.4 = ((bf16[48,2,384]{2,1,0:T(2,128)(2,1)}), bf16[48,2,384]{2,1,0:T(2,128)(2,1)}, u32[]{:S(2)}, u32[]{:S(2)}) async-start(bf16[48,2,384]{2,1,0:T(2,128)(2,1)} %reshape.1603), calls=%async_computation.4 | async-start | bytes 147456 | tf_op jit(solution)/shard_map/all_to_all | solution.py:116
  (86 other events, 54.3 us)
where the time goes:
time: 1050 us; the launch traced here: 1030 us
  other arithmetic  485 us (46%)
  local copies, waits for them, and re-layouts  225 us (21%)
  loops' own time  123 us (12%)
  starting transfers between devices  98.8 us (9%)
  waiting for transfers between devices  39.7 us (4%)
  matrix products  30 us (3%)
  blocking collectives  27.8 us (3%)
    while x180, other arithmetic  245 us
    eq x192, other arithmetic, advance(): degree == order_i  128 us
    another operation x1, loops' own time, legendre_table(): lax.scan(advance, (zero_rows, zero_rows), jnp.arange(amount, dtype=jnp.in...  123 us
    sqrt x108, other arithmetic, advance(): jnp.sqrt(jnp.maximum(prior * prior - order_f * order_f, 0.0) / jnp.maximu...  57.3 us
    unnamed x57, local copies, waits for them, and re-layouts  37.6 us
    ppermute x4, starting transfers between devices, extended(): after = lax.ppermute(first, axis, down)  33.8 us
    reshape x18, local copies, waits for them, and re-layouts, conv_taps(): padded[row_tap:row_tap + row_count, col_tap:col_tap + col_count]  29.2 us
    all_to_all x1, blocking collectives, to_channels(): lax.all_to_all(values, 'lon', split_axis=0, concat_axis=2, tiled=True)  27.8 us
  transfers between devices with their start and end apart: 13, of which 6 were waited for; matrix products, arithmetic and copies ran while one was open for 52% of the time, Pallas kernels for 0%

commit v1 on v0

v1 whole, which is shorter than its diff:
```python
import functools
import math

import jax
import jax.numpy as jnp
import numpy as np
from jax import lax
from jax.experimental import pallas as pl
from jax.experimental.pallas import tpu as pltpu
from jax.sharding import PartitionSpec as P

EPS = 1e-06
C = 384
LANES = 128
THIRDS = 3
ROWS, COLS = 12, 15
PAD = 16
LAT, LON = 16, 48
NLAT, NLON = 192, 720
MODES = 192
OWN = 4
F32, BF16 = jnp.float32, jnp.bfloat16


def lon_tables():
    m = (OWN * np.arange(LON)[:, None, None] + np.arange(OWN)[None, None, :]) + np.zeros((1, 2, 1), int)
    part = np.zeros((LON, 1, OWN), int) + np.arange(2)[None, :, None]
    m, part = m.reshape(-1), part.reshape(-1)
    j = COLS * np.arange(LON)[:, None] + np.arange(PAD)[None, :]
    held = np.broadcast_to(np.arange(PAD)[None, :] < COLS, j.shape).reshape(-1)
    j = j.reshape(-1)
    phase = (m[:, None] * j[None, :] % NLON) * (2.0 * math.pi / NLON)
    wave = np.where(part[:, None] == 0, np.cos(phase), -np.sin(phase)) * held[None, :]
    forward = wave * (2.0 * math.pi / NLON)
    inverse = (wave * np.where(m == 0, 1.0, 2.0)[:, None]).T
    return jnp.asarray(forward, BF16), jnp.asarray(inverse, BF16)


def padded_rows(values):
    blocks = values.reshape(*values.shape[:-1], LAT, ROWS)
    spare = [(0, 0)] * (blocks.ndim - 1) + [(0, PAD - ROWS)]
    return np.pad(blocks, spare).reshape(*values.shape[:-1], LAT * PAD)


def lat_tables():
    m = np.arange(MODES)[:, None].astype(np.float64)
    l = np.arange(MODES)[None, :].astype(np.float64)
    growth = np.sqrt(np.maximum(4 * l * l - 1, 1) / np.maximum(l * l - m * m, 1))
    prior = l - 1
    damping = np.sqrt(np.maximum(prior * prior - m * m, 0) / np.maximum(4 * prior * prior - 1, 1))
    theta = (np.arange(NLAT) + 0.5) * (math.pi / NLAT)
    gam = np.array([math.lgamma(k + 0.5) - math.lgamma(k + 1.0) for k in range(MODES)])[:, None]
    log_start = 0.5 * (np.log((2 * m + 1) / (4 * math.pi)) + gam - 0.5 * math.log(math.pi))
    sectoral = np.exp(log_start + m * np.log(np.sin(theta))[None, :])
    cosine = padded_rows(np.cos(theta)[None, :])
    weight = padded_rows((np.sin(theta) * (math.pi / NLAT))[None, :])
    return (
        np.stack([growth, damping], 1).astype(np.float32),
        padded_rows(sectoral)[:, None, :].astype(np.float32),
        np.concatenate([cosine, weight], 0).astype(np.float32),
    )


def gelu(value):
    return 0.5 * value * (1.0 + lax.erf(value * math.sqrt(0.5)))


def legendre_kernel(order_ref, coeff_ref, start_ref, rows_ref, weighted_ref, turned_ref, table):
    order = order_ref[0]
    cosine = rows_ref[0:1, :]
    start = start_ref[...]
    table[...] = jnp.zeros_like(table)

    def block(step, carry):
        before, latest = carry
        for inner in range(ROWS):
            degree = step * ROWS + inner
            grown = coeff_ref[0, degree] * (cosine * latest - coeff_ref[1, degree] * before)
            fresh = jnp.where(
                degree < order, jnp.zeros_like(grown), jnp.where(degree == order, start, grown)
            )
            table[pl.ds(step * PAD + inner, 1), :] = fresh
            before, latest = latest, fresh
        return before, latest

    zero = jnp.zeros_like(start)
    lax.fori_loop(0, LAT, block, (zero, zero))
    values = table[...]
    weighted_ref[...] = (values * rows_ref[1:2, :]).astype(BF16)
    turned_ref[...] = values.T.astype(BF16)


def legendre(order):
    coefficients, starts, rows = lat_tables()
    coefficient = lax.dynamic_index_in_dim(jnp.asarray(coefficients), order, 0, False)
    start = lax.dynamic_index_in_dim(jnp.asarray(starts), order, 0, False)
    side = LAT * PAD
    return pl.pallas_call(
        legendre_kernel,
        name="legendre",
        out_shape=[jax.ShapeDtypeStruct((side, side), BF16)] * 2,
        in_specs=[
            pl.BlockSpec(memory_space=pltpu.SMEM),
            pl.BlockSpec(memory_space=pltpu.SMEM),
            pl.BlockSpec(memory_space=pltpu.VMEM),
            pl.BlockSpec(memory_space=pltpu.VMEM),
        ],
        out_specs=[pl.BlockSpec(memory_space=pltpu.VMEM)] * 2,
        scratch_shapes=[pltpu.VMEM((side, side), F32)],
        cost_estimate=pl.CostEstimate(flops=6_000_000, bytes_accessed=300_000, transcendentals=0),
    )(order[None], coefficient, start, jnp.asarray(rows))


def conv_kernel(
    place_ref, x_ref, top_ref, bottom_ref, left_ref, right_ref, gain_ref, weight_ref,
    held_ref, send_ref,
    raw, normed, taps, weights, mid, sems,
):
    copies = []
    for layer in range(2):
        for col in range(3):
            for row in range(3):
                copy = pltpu.make_async_copy(
                    weight_ref.at[layer, row, col],
                    weights.at[layer, col, pl.ds(row * C, C)],
                    sems.at[layer, col, row],
                )
                copy.start()
                copies.append(copy)

    def place_line(start, count, line):
        for third in range(THIRDS):
            raw[third, pl.ds(start, count, stride=PAD), :] = line[
                :, third * LANES : (third + 1) * LANES
            ]

    def raw_lines(start, count):
        return jnp.concatenate([raw[t, start : start + count, :] for t in range(THIRDS)], axis=1)

    for row in range(ROWS):
        place_line(2 * PAD + row + 2, COLS, x_ref[row])
    for row in range(2):
        place_line(2 * PAD + row, COLS, top_ref[row])
        place_line(2 * PAD + ROWS + 2 + row, COLS, bottom_ref[row])
    for row in range(PAD):
        place_line(row, 2, left_ref[row])
        place_line((2 + COLS) * PAD + row, 2, right_ref[row])

    def scaled(value, layer):
        scale = lax.rsqrt(jnp.mean(value * value, axis=-1, keepdims=True) + EPS)
        return value * scale * gain_ref[layer : layer + 1, :]

    def convolved(layer, count):
        for row in range(3):
            taps[0 : count + 2 * PAD, row * C : (row + 1) * C] = normed[
                row : row + count + 2 * PAD, :
            ].astype(BF16)
        total = None
        for col in range(3):
            for row in range(3):
                copies[(layer * 3 + col) * 3 + row].wait()
            part = jnp.dot(
                taps[col * PAD : col * PAD + count, :],
                weights[layer, col],
                preferred_element_type=F32,
            )
            total = part if total is None else total + part
        return total

    first, second = (COLS + 2) * PAD, COLS * PAD
    tail = jnp.zeros((8, C), F32)
    normed[0 : first + 2 * PAD, :] = scaled(raw_lines(0, first + 2 * PAD), 0)
    normed[first + 2 * PAD : first + 2 * PAD + 8, :] = tail
    mid[...] = raw_lines(PAD + 1, first) + gelu(convolved(0, first))
    row = lax.broadcasted_iota(jnp.int32, (first, 1), 0) % PAD
    outside = ((row == 0) & (place_ref[0] == 0)) | ((row == ROWS + 1) & (place_ref[0] == LAT - 1))
    normed[0:first, :] = jnp.where(outside, 0.0, scaled(mid[...], 1))
    normed[first : first + 8, :] = tail
    last = mid[PAD + 1 : PAD + 1 + second, :] + gelu(convolved(1, second))
    for third in range(THIRDS):
        raw[third, 0:second, :] = last[:, third * LANES : (third + 1) * LANES]
        raw[third, second : second + PAD, :] = jnp.zeros((PAD, LANES), F32)
    for row in range(ROWS):
        for third in range(THIRDS):
            line = raw[third, pl.ds(row, PAD, stride=PAD), :]
            held_ref[row, :, third * LANES : (third + 1) * LANES] = line
            send_ref[row * THIRDS + third] = line.astype(BF16)
    send_ref[ROWS * THIRDS :] = jnp.zeros((LON - ROWS * THIRDS, PAD, LANES), BF16)


def convolutions(place, x, top, bottom, left, right, gain, weight):
    spots = (COLS + 4) * PAD
    vmem = pl.BlockSpec(memory_space=pltpu.VMEM)
    return pl.pallas_call(
        conv_kernel,
        name="convolutions",
        out_shape=[
            jax.ShapeDtypeStruct((ROWS, PAD, C), F32),
            jax.ShapeDtypeStruct((LON, PAD, LANES), BF16),
        ],
        in_specs=[pl.BlockSpec(memory_space=pltpu.SMEM)] + [vmem] * 6 + [pl.BlockSpec(memory_space=pl.ANY)],
        out_specs=[vmem, vmem],
        scratch_shapes=[
            pltpu.VMEM((THIRDS, spots, LANES), F32),
            pltpu.VMEM((spots + 8, C), F32),
            pltpu.VMEM((spots, 3 * C), BF16),
            pltpu.VMEM((2, 3, 3 * C, C), BF16),
            pltpu.VMEM(((COLS + 2) * PAD, C), F32),
            pltpu.SemaphoreType.DMA((2, 3, 3)),
        ],
        cost_estimate=pl.CostEstimate(
            flops=2 * 512 * 9 * C * C, bytes_accessed=6_500_000, transcendentals=200_000
        ),
    )(place[None], x, top, bottom, left, right, gain, weight)


def spread_kernel(in_ref, out_ref, held):
    held[...] = in_ref[...].astype(F32).reshape(LON * 8, LANES)
    for third in range(THIRDS):
        for order in range(OWN):
            parts = [
                held[pl.ds(third * 8 + part * OWN + order, PAD, stride=THIRDS * 8), :].astype(BF16)
                for part in range(2)
            ]
            out_ref[third * OWN + order] = jnp.concatenate(parts, axis=1)
    out_ref[THIRDS * OWN :] = jnp.zeros((LAT - THIRDS * OWN, PAD, 2 * LANES), BF16)


def gather_kernel(in_ref, out_ref, held):
    for third in range(THIRDS):
        for order in range(OWN):
            block = in_ref[third * OWN + order].astype(F32)
            for part in range(2):
                held[pl.ds(third * 8 + part * OWN + order, PAD, stride=THIRDS * 8), :] = block[
                    :, part * LANES : (part + 1) * LANES
                ]
    out_ref[...] = held[...].reshape(LON, 8, LANES).astype(BF16)


def reshuffled(kernel, name, shape, data):
    vmem = pl.BlockSpec(memory_space=pltpu.VMEM)
    return pl.pallas_call(
        kernel,
        name=name,
        out_shape=jax.ShapeDtypeStruct(shape, BF16),
        in_specs=[vmem],
        out_specs=vmem,
        scratch_shapes=[pltpu.VMEM((LON * 8, LANES), F32)],
        cost_estimate=pl.CostEstimate(flops=1_000_000, bytes_accessed=250_000, transcendentals=0),
    )(data)


def filter_kernel(in_ref, keep_ref, weight_ref, out_ref, given, made, weights, sems):
    copies = []
    for degree in range(ROWS):
        copy = pltpu.make_async_copy(weight_ref.at[degree], weights.at[degree], sems.at[degree])
        copy.start()
        copies.append(copy)
    for part in range(2):
        given[part] = (
            in_ref[:, :, part * LANES : (part + 1) * LANES].astype(F32).reshape(LAT * PAD, LANES)
        )
    made[...] = jnp.zeros_like(made)
    for degree in range(ROWS):
        lines = [
            jnp.concatenate(
                [
                    given[part, pl.ds(third * OWN * PAD + degree, OWN, stride=PAD), :]
                    for third in range(THIRDS)
                ],
                axis=1,
            )
            for part in range(2)
        ]
        lines = jnp.concatenate(lines, axis=0).astype(BF16)
        copies[degree].wait()
        mixed = jnp.dot(lines, weights[degree], preferred_element_type=F32)
        for third in range(THIRDS):
            piece = mixed[:, third * LANES : (third + 1) * LANES] * keep_ref[degree]
            for part in range(2):
                made[part, pl.ds(third * OWN * PAD + degree, OWN, stride=PAD), :] = piece[
                    part * OWN : (part + 1) * OWN
                ]
    for part in range(2):
        out_ref[:, :, part * LANES : (part + 1) * LANES] = (
            made[part].reshape(LAT, PAD, LANES).astype(BF16)
        )


def filtered(data, keep, weight):
    vmem = pl.BlockSpec(memory_space=pltpu.VMEM)
    lines = jnp.concatenate([keep, keep], axis=1).astype(F32)[:, :, None]
    lines = jnp.broadcast_to(lines, (ROWS, 2 * OWN, LANES))
    return pl.pallas_call(
        filter_kernel,
        name="filter",
        out_shape=jax.ShapeDtypeStruct(data.shape, BF16),
        in_specs=[vmem, vmem, pl.BlockSpec(memory_space=pl.ANY)],
        out_specs=vmem,
        scratch_shapes=[
            pltpu.VMEM((2, LAT * PAD, LANES), F32),
            pltpu.VMEM((2, LAT * PAD, LANES), F32),
            pltpu.VMEM((ROWS, C, C), BF16),
            pltpu.SemaphoreType.DMA((ROWS,)),
        ],
        cost_estimate=pl.CostEstimate(
            flops=2 * ROWS * 128 * C * C, bytes_accessed=4_000_000, transcendentals=0
        ),
    )(data, lines, weight)


def finish_kernel(held_ref, in_ref, out_ref):
    for row in range(ROWS):
        physical = jnp.concatenate([in_ref[row * THIRDS + t] for t in range(THIRDS)], axis=1)
        value = held_ref[row] + gelu(physical.astype(F32))
        out_ref[row] = value[:COLS]


def finished(held, physical):
    vmem = pl.BlockSpec(memory_space=pltpu.VMEM)
    return pl.pallas_call(
        finish_kernel,
        name="finish",
        out_shape=jax.ShapeDtypeStruct((ROWS, COLS, C), F32),
        in_specs=[vmem, vmem],
        out_specs=vmem,
        cost_estimate=pl.CostEstimate(flops=3_000_000, bytes_accessed=800_000, transcendentals=70_000),
    )(held, physical)


def exchange(data, axis):
    return lax.all_to_all(data, axis, 0, 0, tiled=True)


def matmul(left, right):
    return jnp.dot(left, right, preferred_element_type=F32).astype(BF16)


def halo(x):
    up = [(i, i + 1) for i in range(LAT - 1)]
    down = [(j, i) for i, j in up]
    top = lax.ppermute(x[ROWS - 2 :], "lat", up)
    bottom = lax.ppermute(x[:2], "lat", down)
    east = [(i, (i + 1) % LON) for i in range(LON)]
    west = [(j, i) for i, j in east]
    last = jnp.concatenate([top[:, -2:], x[:, -2:], bottom[:, -2:]], axis=0)
    first = jnp.concatenate([top[:, :2], x[:, :2], bottom[:, :2]], axis=0)
    left = lax.ppermute(last, "lon", east)
    right = lax.ppermute(first, "lon", west)
    return top, bottom, left, right


def per_device(grid_state, norm_gain, conv_weight, filter_weight, degree_keep):
    lat, lon = lax.axis_index("lat"), lax.axis_index("lon")
    side = LAT * PAD
    forward, inverse = lon_tables()
    analysis, synthesis = legendre(lon * OWN + lat % OWN)
    edges = halo(grid_state)
    held, data = convolutions(lat, grid_state, *edges, norm_gain, conv_weight)
    data = exchange(data, "lon").reshape(LON * PAD, LANES)
    data = exchange(matmul(forward, data).reshape(LON, 8, LANES), "lon")
    data = reshuffled(spread_kernel, "spread", (LAT, PAD, 2 * LANES), data)
    data = exchange(data, "lat").reshape(side, 2 * LANES)
    data = exchange(matmul(analysis, data).reshape(LAT, PAD, 2 * LANES), "lat")
    data = filtered(data, degree_keep, filter_weight)
    data = exchange(data, "lat").reshape(side, 2 * LANES)
    data = exchange(matmul(synthesis, data).reshape(LAT, PAD, 2 * LANES), "lat")
    data = reshuffled(gather_kernel, "gather", (LON, 8, LANES), data)
    data = exchange(data, "lon").reshape(LON * 8, LANES)
    data = exchange(matmul(inverse, data).reshape(LON, PAD, LANES), "lon")
    return finished(held, data)


def solution(mesh):
    in_specs = (P("lat", "lon", None), P(), P(), P("lat", None, None), P("lat", "lon"))
    return jax.shard_map(
        per_device, mesh=mesh, in_specs=in_specs, out_specs=P("lat", "lon", None), check_vma=False
    )
```

time: 1050 us -> 199 us (0.19); the launches traced: 1030 us -> 198 us
  other arithmetic: 485 us -> 0.06 us
  local copies, waits for them, and re-layouts: 225 us -> 6.14 us
  loops' own time: 123 us -> 0 us
  blocking collectives: 27.8 us -> 128 us
  starting transfers between devices: 98.8 us -> 27.5 us
  matrix products: 30 us -> 3.49 us
  waiting for transfers between devices: 39.7 us -> 13.8 us
  Pallas kernels: 0 us -> 18.7 us
    while x180 -> x0, other arithmetic: 245 us -> none
    eq x192 -> x0, other arithmetic: 128 us -> none  [advance(): degree == order_i]
    another operation x1 -> x0, loops' own time: 123 us -> none  [legendre_table(): lax.scan(advance, (zero_rows, zero_rows), jnp.arange(amount, dtype=jnp.in...]
    all_to_all x1 -> x6, blocking collectives: 27.8 us -> 128 us  [exchange(): return lax.all_to_all(data, axis, 0, 0, tiled=True)]
    sqrt x192 -> x0, other arithmetic: 58.6 us -> none  [the longest x108 57.3 us: advance(): jnp.sqrt(jnp.maximum(prior * prior - order_f * order_f, 0.0) / jnp.maximu...]
    reshape x25 -> x0, local copies, waits for them, and re-layouts: 44.9 us -> none  [the longest x18 29.2 us: conv_taps(): padded[row_tap:row_tap + row_count, col_tap:col_tap + col_count]]
    all_to_all x5 -> x2, starting transfers between devices: 51.8 us -> 9.44 us  [exchange(): return lax.all_to_all(data, axis, 0, 0, tiled=True)]
    unnamed x57 -> x16, local copies, waits for them, and re-layouts: 37.6 us -> 0.63 us
  transfers between devices with their start and end apart: 13 -> 6, of which waited for: 6 -> 4; matrix products, arithmetic and copies ran while one was open for 52% -> 2% of each run, Pallas kernels for 0% -> 1%
where the time goes in v1:
time: 199 us; the launch traced here: 198 us
  blocking collectives  128 us (64%)
  starting transfers between devices  27.5 us (14%)
  Pallas kernels  18.7 us (9%)
  waiting for transfers between devices  13.8 us (7%)
  local copies, waits for them, and re-layouts  6.14 us (3%)
  matrix products  3.49 us (2%)
    all_to_all x6, blocking collectives, exchange(): return lax.all_to_all(data, axis, 0, 0, tiled=True)  128 us
    all_to_all x2, waiting for transfers between devices, exchange(): return lax.all_to_all(data, axis, 0, 0, tiled=True)  10.4 us
    all_to_all x2, starting transfers between devices, exchange(): return lax.all_to_all(data, axis, 0, 0, tiled=True)  9.44 us
    ppermute x1, starting transfers between devices, halo(): right = lax.ppermute(first, 'lon', west)  6.82 us
    pallas_call x1, Pallas kernels, convolutions(): pl.pallas_call(conv_kernel, name='convolutions', out_shape=[jax.ShapeDtyp...  6.44 us
    ppermute x1, starting transfers between devices, halo(): left = lax.ppermute(last, 'lon', east)  5.99 us
    pallas_call x1, Pallas kernels, filtered(): pl.pallas_call(filter_kernel, name='filter', out_shape=jax.ShapeDtypeStru...  4.72 us
  transfers between devices with their start and end apart: 6, of which 4 were waited for; matrix products, arithmetic and copies ran while one was open for 2% of the time, Pallas kernels for 1%

profile of v1, /device:TPU:1, one launch (start us, length us, event | category | flops | bytes accessed | tf_op | source)
XLA Modules:
  0.0 197.7 jit_solution(9385997786695828657)
XLA Ops:
  0.0 0.9 fusion.4
  0.9 3.9 %collective-permute-start = (f32[2,15,384]{2,1,0:T(8,128)S(1)}, f32[2,15,384]{2,1,0:T(8,128)S(1)}, u32[]{:S(2)}, u32[]{:S(2)}) collective-permute-start(f32[2,15,384]{2,1,0:T(8,128)S(1)} %get-tuple-element.16), channel_id=1, source_target_pairs={{0,48},{48,96},{96,144},{144,192},{192,240},{240,288},{288,336},{3... | collective-permute-start | bytes 138248 | tf_op jit(solution)/shard_map/ppermute | solution.py:342
  4.8 1.3 collective-permute-start.1
  6.1 1.0 fusion.3
  7.1 2.5 %collective-permute-done.1.bottom_ref = f32[2,15,384]{2,1,0:T(8,128)S(1)} collective-permute-done((f32[2,15,384]{2,1,0:T(8,128)S(1)}, f32[2,15,384]{2,1,0:T(8,128)S(1)}, u32[]{:S(2)}, u32[]{:S(2)}) %collective-permute-start.1) | collective-permute-done | bytes 46112 | tf_op jit(solution)/shard_map/ppermute | solution.py:343
  9.7 6.0 %collective-permute-start.2 = (f32[16,2,384]{2,1,0:T(2,128)S(1)}, f32[16,2,384]{2,1,0:T(2,128)S(1)}, u32[]{:S(2)}, u32[]{:S(2)}) collective-permute-start(f32[16,2,384]{2,1,0:T(2,128)S(1)} %pad_maximum_fusion), channel_id=1, source_target_pairs={{0,1},{1,2},{2,3},{3,4},{4,5},{5,6},{6,7},{7,8},{8,9},{9,10},{10,1... | collective-permute-start | bytes 147464 | tf_op jit(solution)/shard_map/ppermute | solution.py:348
  15.8 6.8 %collective-permute-start.3 = (f32[16,2,384]{2,1,0:T(2,128)S(1)}, f32[16,2,384]{2,1,0:T(2,128)S(1)}, u32[]{:S(2)}, u32[]{:S(2)}) collective-permute-start(f32[16,2,384]{2,1,0:T(2,128)S(1)} %pad_maximum_fusion.1), channel_id=1, source_target_pairs={{1,0},{2,1},{3,2},{4,3},{5,4},{6,5},{7,6},{8,7},{9,8},{10,9},{11,1... | collective-permute-start | bytes 147464 | tf_op jit(solution)/shard_map/ppermute | solution.py:349
  22.6 0.8 collective-permute-done.3.right_ref
  23.5 0.6 copy-done.6
  24.1 6.4 %convolutions.1 = (f32[12,16,384]{2,1,0:T(8,128)}, bf16[48,16,128]{2,1,0:T(8,128)(2,1)}) custom-call(s32[1]{0:T(128)} %bitcast.place_ref, f32[12,15,384]{2,1,0:T(8,128)} %x_ref.1, f32[2,15,384]{2,1,0:T(8,128)} %copy-done.3, f32[2,15,384]{2,1,0:T(8,128)} %copy-done.4, f32[16,2,384]{2,1,0:T(2,128)} %copy-done.5, f32[16,2,384]{2,1,0:T(2,128)} %copy-done.6, ...), custom_call_target="tpu_custom_call" | custom-call | flops 1358954496 | bytes 6500000 | tf_op jit(solution)/shard_map/convolutions/pallas_call | solution.py:194
  30.5 37.3 %all_to_all.40 = bf16[48,16,128]{2,1,0:T(8,128)(2,1)S(1)} all-to-all(bf16[48,16,128]{2,1,0:T(8,128)(2,1)} %get-tuple-element.12), channel_id=1, replica_groups=mesh['lat'=16,'lon'=48] {'lon'}, dimensions={0} | all-to-all | bytes 393216 | tf_op jit(solution)/shard_map/all_to_all | solution.py:332
  67.8 0.3 fusion.1
  68.3 21.3 %all_to_all.41.in_ref = bf16[48,8,128]{2,1,0:T(8,128)(2,1)} all-to-all(bf16[48,8,128]{2,1,0:T(8,128)(2,1)S(1)} %bitcast.32), channel_id=1, replica_groups=mesh['lat'=16,'lon'=48] {'lon'}, dimensions={0} | all-to-all | bytes 196608 | tf_op jit(solution)/shard_map/all_to_all | solution.py:332
  89.5 1.6 spread.1
  91.1 5.1 %all-to-all-start.2 = ((bf16[16,16,256]{2,1,0:T(8,128)(2,1)}), bf16[16,16,256]{2,1,0:T(8,128)(2,1)S(1)}, u32[]{:S(2)}, u32[]{:S(2)}) async-start(bf16[16,16,256]{2,1,0:T(8,128)(2,1)} %spread.1), calls=%async_computation.2 | async-start | bytes 262144 | tf_op jit(solution)/shard_map/all_to_all | solution.py:332
  96.3 1.3 dynamic-slice_bitcast_fusion.1.start_ref
  97.6 1.3 dynamic-slice_bitcast_fusion.coeff_ref
  98.9 2.6 %legendre.1 = (bf16[256,256]{1,0:T(8,128)(2,1)}, bf16[256,256]{1,0:T(8,128)(2,1)}) custom-call(s32[1]{0:T(128)} %bitcast.1.order_ref, f32[2,192]{1,0:T(2,128)} %dynamic-slice_bitcast_fusion.coeff_ref, f32[1,256]{1,0:T(1,128)} %dynamic-slice_bitcast_fusion.1.start_ref, f32[2,256]{1,0:T(2,128)} %constant.42.clone.rows_ref), custom_call_target="tpu_custom_call" | custom-call | flops 6000000 | bytes 300000 | tf_op jit(solution)/shard_map/legendre/pallas_call | solution.py:98
  101.4 2.6 %all-to-all-done.2 = bf16[16,16,256]{2,1,0:T(8,128)(2,1)S(1)} async-done(((bf16[16,16,256]{2,1,0:T(8,128)(2,1)}), bf16[16,16,256]{2,1,0:T(8,128)(2,1)S(1)}, u32[]{:S(2)}, u32[]{:S(2)}) %all-to-all-start.2) | async-done | bytes 131104 | tf_op jit(solution)/shard_map/all_to_all | solution.py:332
  104.1 1.7 convolution_convert_fusion.2
  105.8 4.3 %all-to-all-start.3 = ((bf16[16,16,256]{2,1,0:T(8,128)(2,1)}), bf16[16,16,256]{2,1,0:T(8,128)(2,1)S(1)}, u32[]{:S(2)}, u32[]{:S(2)}) async-start(bf16[16,16,256]{2,1,0:T(8,128)(2,1)} %bitcast.8), calls=%async_computation.3 | async-start | bytes 262144 | tf_op jit(solution)/shard_map/all_to_all | solution.py:332
  110.2 7.8 %all-to-all-done.3.in_ref = bf16[16,16,256]{2,1,0:T(8,128)(2,1)S(1)} async-done(((bf16[16,16,256]{2,1,0:T(8,128)(2,1)}), bf16[16,16,256]{2,1,0:T(8,128)(2,1)S(1)}, u32[]{:S(2)}, u32[]{:S(2)}) %all-to-all-start.3) | async-done | bytes 131104 | tf_op jit(solution)/shard_map/all_to_all | solution.py:332
  118.0 0.7 broadcast_in_dim.14.keep_ref
  118.7 4.7 %filter.1 = bf16[16,16,256]{2,1,0:T(8,128)(2,1)} custom-call(bf16[16,16,256]{2,1,0:T(8,128)(2,1)} %copy-done.2, f32[12,8,128]{2,1,0:T(8,128)} %broadcast_in_dim.14.keep_ref, bf16[12,384,384]{2,1,0:T(8,128)(2,1)} %weight_ref.3), custom_call_target="tpu_custom_call" | custom-call | flops 452984832 | bytes 4000000 | tf_op jit(solution)/shard_map/filter/pallas_call | solution.py:294
  123.4 11.4 %all_to_all.42 = bf16[16,16,256]{2,1,0:T(8,128)(2,1)S(1)} all-to-all(bf16[16,16,256]{2,1,0:T(8,128)(2,1)} %filter.1), channel_id=1, replica_groups=mesh['lat'=16,'lon'=48] {'lat'}, dimensions={0} | all-to-all | bytes 262144 | tf_op jit(solution)/shard_map/all_to_all | solution.py:332
  134.8 1.1 convolution_convert_fusion.1
  135.9 11.0 %all_to_all.43.in_ref = bf16[16,16,256]{2,1,0:T(8,128)(2,1)} all-to-all(bf16[16,16,256]{2,1,0:T(8,128)(2,1)S(1)} %bitcast.31), channel_id=1, replica_groups=mesh['lat'=16,'lon'=48] {'lat'}, dimensions={0} | all-to-all | bytes 262144 | tf_op jit(solution)/shard_map/all_to_all | solution.py:332
  146.9 1.6 gather.1
  148.5 24.8 %all_to_all.44 = bf16[48,8,128]{2,1,0:T(8,128)(2,1)S(1)} all-to-all(bf16[48,8,128]{2,1,0:T(8,128)(2,1)} %gather.1), channel_id=1, replica_groups=mesh['lat'=16,'lon'=48] {'lon'}, dimensions={0} | all-to-all | bytes 196608 | tf_op jit(solution)/shard_map/all_to_all | solution.py:332
  173.3 0.3 fusion
  173.8 22.1 %all_to_all.45.in_ref = bf16[48,16,128]{2,1,0:T(8,128)(2,1)} all-to-all(bf16[48,16,128]{2,1,0:T(8,128)(2,1)S(1)} %bitcast.28), channel_id=1, replica_groups=mesh['lat'=16,'lon'=48] {'lon'}, dimensions={0} | all-to-all | bytes 393216 | tf_op jit(solution)/shard_map/all_to_all | solution.py:332
  195.9 1.8 finish.1
  (25 shorter events, 0.5 us)
Async XLA Ops:
  0.0 67.8 %copy-start.1 = (bf16[384,768]{1,0:T(8,128)(2,1)S(1)}, bf16[384,768]{1,0:T(8,128)(2,1)}, u32[]{:S(2)}) copy-start(bf16[384,768]{1,0:T(8,128)(2,1)} %constant.38.clone) | copy-start | bytes 1769476
  0.0 110.1 %copy-start.7 = (s32[12,4]{0,1:T(4,128)S(1)}, s32[12,4]{0,1:T(4,128)}, u32[]{:S(2)}) copy-start(s32[12,4]{0,1:T(4,128)} %param.14) | copy-start | bytes 580
  0.9 8.8 %collective-permute-start = (f32[2,15,384]{2,1,0:T(8,128)S(1)}, f32[2,15,384]{2,1,0:T(8,128)S(1)}, u32[]{:S(2)}, u32[]{:S(2)}) collective-permute-start(f32[2,15,384]{2,1,0:T(8,128)S(1)} %get-tuple-element.16), channel_id=1, source_target_pairs={{0,48},{48,96},{96,144},{144,192},{192,240},{240,288},{288,336},{3... | collective-permute-start | bytes 138248 | tf_op jit(solution)/shard_map/ppermute | solution.py:342
  4.8 4.8 %collective-permute-start.1 = (f32[2,15,384]{2,1,0:T(8,128)S(1)}, f32[2,15,384]{2,1,0:T(8,128)S(1)}, u32[]{:S(2)}, u32[]{:S(2)}) collective-permute-start(f32[2,15,384]{2,1,0:T(8,128)S(1)} %get-tuple-element.15), channel_id=1, source_target_pairs={{48,0},{96,48},{144,96},{192,144},{240,192},{288,240},{336,288},{3... | collective-permute-start | bytes 138248 | tf_op jit(solution)/shard_map/ppermute | solution.py:343
  9.7 13.8 %copy-start.4 = (f32[2,15,384]{2,1,0:T(8,128)}, f32[2,15,384]{2,1,0:T(8,128)S(1)}, u32[]{:S(2)}) copy-start(f32[2,15,384]{2,1,0:T(8,128)S(1)} %collective-permute-done.1.bottom_ref) | copy-start | bytes 138244
  9.7 13.8 %copy-start.3 = (f32[2,15,384]{2,1,0:T(8,128)}, f32[2,15,384]{2,1,0:T(8,128)S(1)}, u32[]{:S(2)}) copy-start(f32[2,15,384]{2,1,0:T(8,128)S(1)} %collective-permute-done.top_ref) | copy-start | bytes 138244
  9.7 12.9 %collective-permute-start.2 = (f32[16,2,384]{2,1,0:T(2,128)S(1)}, f32[16,2,384]{2,1,0:T(2,128)S(1)}, u32[]{:S(2)}, u32[]{:S(2)}) collective-permute-start(f32[16,2,384]{2,1,0:T(2,128)S(1)} %pad_maximum_fusion), channel_id=1, source_target_pairs={{0,1},{1,2},{2,3},{3,4},{4,5},{5,6},{6,7},{7,8},{8,9},{9,10},{10,1... | collective-permute-start | bytes 147464 | tf_op jit(solution)/shard_map/ppermute | solution.py:348
  15.8 7.7 %collective-permute-start.3 = (f32[16,2,384]{2,1,0:T(2,128)S(1)}, f32[16,2,384]{2,1,0:T(2,128)S(1)}, u32[]{:S(2)}, u32[]{:S(2)}) collective-permute-start(f32[16,2,384]{2,1,0:T(2,128)S(1)} %pad_maximum_fusion.1), channel_id=1, source_target_pairs={{1,0},{2,1},{3,2},{4,3},{5,4},{6,5},{7,6},{8,7},{9,8},{10,9},{11,1... | collective-permute-start | bytes 147464 | tf_op jit(solution)/shard_map/ppermute | solution.py:349
  22.6 0.9 copy-start.5
  23.5 0.6 copy-start.6
  30.5 142.8 %copy-start = (bf16[768,384]{1,0:T(8,128)(2,1)S(1)}, bf16[768,384]{1,0:T(8,128)(2,1)}, u32[]{:S(2)}) copy-start(bf16[768,384]{1,0:T(8,128)(2,1)} %constant.39.clone) | copy-start | bytes 1769476
  91.1 12.9 %all-to-all-start.2 = ((bf16[16,16,256]{2,1,0:T(8,128)(2,1)}), bf16[16,16,256]{2,1,0:T(8,128)(2,1)S(1)}, u32[]{:S(2)}, u32[]{:S(2)}) async-start(bf16[16,16,256]{2,1,0:T(8,128)(2,1)} %spread.1), calls=%async_computation.2 | async-start | bytes 262144 | tf_op jit(solution)/shard_map/all_to_all | solution.py:332
  105.8 12.2 %all-to-all-start.3 = ((bf16[16,16,256]{2,1,0:T(8,128)(2,1)}), bf16[16,16,256]{2,1,0:T(8,128)(2,1)S(1)}, u32[]{:S(2)}, u32[]{:S(2)}) async-start(bf16[16,16,256]{2,1,0:T(8,128)(2,1)} %bitcast.8), calls=%async_computation.3 | async-start | bytes 262144 | tf_op jit(solution)/shard_map/all_to_all | solution.py:332
  118.0 0.7 copy-start.2

commit v2 on v1

v2 whole, which is shorter than its diff:
```python
import functools
import math

import jax
import jax.numpy as jnp
import numpy as np
from jax import lax
from jax.experimental import pallas as pl
from jax.experimental.pallas import tpu as pltpu
from jax.sharding import PartitionSpec as P

EPS = 1e-06
C = 384
LANES = 128
THIRDS = 3
ROWS, COLS = 12, 15
PAD = 16
LAT, LON = 16, 48
NLAT, NLON = 192, 720
MODES = 192
SLOTS = 16
PER = 4
F32, BF16 = jnp.float32, jnp.bfloat16


def lon_of(slot, third):
    return (slot // 8 * 12 + slot // 2 % 4 * THIRDS + third) * 2 + slot % 2


ORDER_GROUPS = [
    [a * LON + lon_of(slot, third) for a in range(LAT) for slot in range(SLOTS)]
    for third in range(THIRDS)
]
DEGREE_GROUPS = [
    [a * LON + lon_of(slot, third) for a in range(LAT) for third in range(THIRDS)]
    for slot in range(SLOTS)
]


def lon_table():
    shape = (LAT, SLOTS, 2)
    m = np.broadcast_to(ROWS * np.arange(SLOTS)[None, :, None] + np.arange(LAT)[:, None, None], shape)
    used = np.broadcast_to(np.arange(LAT)[:, None, None] < ROWS, shape).reshape(-1)
    part = np.broadcast_to(np.arange(2)[None, None, :], shape).reshape(-1)
    m = m.reshape(-1)
    j = COLS * np.arange(LON)[:, None] + np.arange(PAD)[None, :]
    held = np.broadcast_to(np.arange(PAD)[None, :] < COLS, j.shape).reshape(-1)
    j = j.reshape(-1)
    phase = (m[:, None] * j[None, :] % NLON) * (2.0 * math.pi / NLON)
    wave = np.where(part[:, None] == 0, np.cos(phase), -np.sin(phase))
    return jnp.asarray(wave * held[None, :] * used[:, None], BF16)


def padded_rows(values):
    blocks = values.reshape(*values.shape[:-1], LAT, ROWS)
    spare = [(0, 0)] * (blocks.ndim - 1) + [(0, PAD - ROWS)]
    return np.pad(blocks, spare).reshape(*values.shape[:-1], LAT * PAD)


def lat_tables():
    m = np.arange(MODES)[:, None].astype(np.float64)
    l = np.arange(MODES)[None, :].astype(np.float64)
    growth = np.sqrt(np.maximum(4 * l * l - 1, 1) / np.maximum(l * l - m * m, 1))
    prior = l - 1
    damping = np.sqrt(np.maximum(prior * prior - m * m, 0) / np.maximum(4 * prior * prior - 1, 1))
    theta = (np.arange(NLAT) + 0.5) * (math.pi / NLAT)
    gam = np.array([math.lgamma(k + 0.5) - math.lgamma(k + 1.0) for k in range(MODES)])[:, None]
    log_start = 0.5 * (np.log((2 * m + 1) / (4 * math.pi)) + gam - 0.5 * math.log(math.pi))
    sectoral = np.exp(log_start + m * np.log(np.sin(theta))[None, :])
    cosine = padded_rows(np.cos(theta)[None, :])
    weight = padded_rows((np.sin(theta) * (math.pi / NLAT))[None, :])
    spare = [(0, 0), (0, LAT * PAD - MODES)]
    table = np.stack([np.pad(growth, spare), np.pad(damping, spare), padded_rows(sectoral)], 1)
    return table.astype(np.float32), np.concatenate([cosine, weight], 0).astype(np.float32)


def gelu(value):
    return 0.5 * value * (1.0 + lax.erf(value * math.sqrt(0.5)))


def legendre_kernel(order_ref, coeff_ref, start_ref, rows_ref, weighted_ref, turned_ref, table):
    order = order_ref[0]
    cosine = rows_ref[0:1, :]
    start = start_ref[2:3, :]

    def block(step, carry):
        before, latest = carry
        for inner in range(PAD):
            degree = step * PAD + inner
            grown = coeff_ref[0, degree] * (cosine * latest - coeff_ref[1, degree] * before)
            fresh = jnp.where(
                degree < order, jnp.zeros_like(grown), jnp.where(degree == order, start, grown)
            )
            table[pl.ds(degree, 1), :] = fresh
            before, latest = latest, fresh
        return before, latest

    zero = jnp.zeros_like(start)
    lax.fori_loop(0, MODES // PAD, block, (zero, zero))
    values = table[...]
    weighted_ref[...] = (values * rows_ref[1:2, :]).astype(BF16)
    turned_ref[...] = (values.T * jnp.where(order == 0, 1.0, 2.0)).astype(BF16)


def legendre(order):
    tables, rows = lat_tables()
    table = lax.dynamic_index_in_dim(jnp.asarray(tables), order, 0, False)
    side = LAT * PAD
    return pl.pallas_call(
        legendre_kernel,
        name="legendre",
        out_shape=[
            jax.ShapeDtypeStruct((MODES, side), BF16),
            jax.ShapeDtypeStruct((side, MODES), BF16),
        ],
        in_specs=[
            pl.BlockSpec(memory_space=pltpu.SMEM),
            pl.BlockSpec(memory_space=pltpu.SMEM),
            pl.BlockSpec(memory_space=pltpu.VMEM),
            pl.BlockSpec(memory_space=pltpu.VMEM),
        ],
        out_specs=[pl.BlockSpec(memory_space=pltpu.VMEM)] * 2,
        scratch_shapes=[pltpu.VMEM((MODES, side), F32)],
        cost_estimate=pl.CostEstimate(flops=6_000_000, bytes_accessed=300_000, transcendentals=0),
    )(order[None], table, table, jnp.asarray(rows))


def conv_kernel(
    place_ref, x_ref, top_ref, bottom_ref, left_ref, right_ref, keep_ref, gain_ref, weight_ref,
    held_ref, send_ref,
    raw, normed, taps, weights, mid, sems,
):
    copies = []
    for layer in range(2):
        for col in range(3):
            for row in range(3):
                copy = pltpu.make_async_copy(
                    weight_ref.at[layer, row, col],
                    weights.at[layer, col, pl.ds(row * C, C)],
                    sems.at[layer, col, row],
                )
                copy.start()
                copies.append(copy)

    def place_line(start, count, line):
        for third in range(THIRDS):
            raw[third, pl.ds(start, count, stride=PAD), :] = line[
                :, third * LANES : (third + 1) * LANES
            ]

    def raw_lines(start, count):
        return jnp.concatenate([raw[t, start : start + count, :] for t in range(THIRDS)], axis=1)

    for row in range(ROWS):
        place_line(2 * PAD + row + 2, COLS, x_ref[row])
    for row in range(2):
        place_line(2 * PAD + row, COLS, top_ref[row])
        place_line(2 * PAD + ROWS + 2 + row, COLS, bottom_ref[row])
    for row in range(PAD):
        place_line(row, 2, left_ref[row])
        place_line((2 + COLS) * PAD + row, 2, right_ref[row])

    def scaled(value, layer):
        scale = lax.rsqrt(jnp.mean(value * value, axis=-1, keepdims=True) + EPS)
        return value * scale * gain_ref[layer : layer + 1, :]

    def convolved(layer, count):
        for row in range(3):
            taps[0 : count + 2 * PAD, row * C : (row + 1) * C] = normed[
                row : row + count + 2 * PAD, :
            ].astype(BF16)
        total = None
        for col in range(3):
            for row in range(3):
                copies[(layer * 3 + col) * 3 + row].wait()
            part = jnp.dot(
                taps[col * PAD : col * PAD + count, :],
                weights[layer, col],
                preferred_element_type=F32,
            )
            total = part if total is None else total + part
        return total

    first, second = (COLS + 2) * PAD, COLS * PAD
    tail = jnp.zeros((8, C), F32)
    normed[0 : first + 2 * PAD, :] = scaled(raw_lines(0, first + 2 * PAD), 0)
    normed[first + 2 * PAD : first + 2 * PAD + 8, :] = tail
    mid[...] = raw_lines(PAD + 1, first) + gelu(convolved(0, first))
    row = lax.broadcasted_iota(jnp.int32, (first, 1), 0) % PAD
    outside = ((row == 0) & (place_ref[0] == 0)) | ((row == ROWS + 1) & (place_ref[0] == LAT - 1))
    normed[0:first, :] = jnp.where(outside, 0.0, scaled(mid[...], 1))
    normed[first : first + 8, :] = tail
    last = mid[PAD + 1 : PAD + 1 + second, :] + gelu(convolved(1, second))
    for third in range(THIRDS):
        raw[third, 0:second, :] = last[:, third * LANES : (third + 1) * LANES]
        raw[third, second : second + PAD, :] = keep_ref[third]
    carried = lax.broadcasted_iota(jnp.int32, (PAD, LANES), 0) == COLS
    for row in range(SLOTS):
        for third in range(THIRDS):
            line = raw[third, pl.ds(row, PAD, stride=PAD), :]
            if row < ROWS:
                held_ref[row, :, third * LANES : (third + 1) * LANES] = line
            else:
                line = jnp.where(carried, line, 0.0)
            send_ref[lon_of(row, third)] = line.astype(BF16)


def convolutions(place, x, top, bottom, left, right, keep, gain, weight):
    spots = (COLS + 4) * PAD
    vmem = pl.BlockSpec(memory_space=pltpu.VMEM)
    return pl.pallas_call(
        conv_kernel,
        name="convolutions",
        out_shape=[
            jax.ShapeDtypeStruct((ROWS, PAD, C), F32),
            jax.ShapeDtypeStruct((LON, PAD, LANES), BF16),
        ],
        in_specs=[pl.BlockSpec(memory_space=pltpu.SMEM)] + [vmem] * 7 + [pl.BlockSpec(memory_space=pl.ANY)],
        out_specs=[vmem, vmem],
        scratch_shapes=[
            pltpu.VMEM((THIRDS, spots, LANES), F32),
            pltpu.VMEM((spots + 8, C), F32),
            pltpu.VMEM((spots, 3 * C), BF16),
            pltpu.VMEM((2, 3, 3 * C, C), BF16),
            pltpu.VMEM(((COLS + 2) * PAD, C), F32),
            pltpu.SemaphoreType.DMA((2, 3, 3)),
        ],
        cost_estimate=pl.CostEstimate(
            flops=2 * 512 * 9 * C * C, bytes_accessed=6_500_000, transcendentals=200_000
        ),
    )(place[None], x, top, bottom, left, right, keep, gain, weight)


def apart(lines, part, count):
    return lines[pl.ds(part, count, stride=2), :]


def lat_kernel(table_ref, in_ref, out_ref, given, made):
    count, depth = table_ref.shape
    given[...] = in_ref[...].astype(F32)
    table = table_ref[...]
    for part in range(2):
        lines = apart(given, part, depth).astype(BF16)
        made[pl.ds(part, count, stride=2), :] = jnp.dot(table, lines, preferred_element_type=F32)
    out_ref[...] = made[...].astype(BF16)


def lat_sums(name, table, data):
    count, depth = table.shape
    vmem = pl.BlockSpec(memory_space=pltpu.VMEM)
    return pl.pallas_call(
        lat_kernel,
        name=name,
        out_shape=jax.ShapeDtypeStruct((2 * count, LANES), BF16),
        in_specs=[vmem, vmem],
        out_specs=vmem,
        scratch_shapes=[pltpu.VMEM((2 * depth, LANES), F32), pltpu.VMEM((2 * count, LANES), F32)],
        cost_estimate=pl.CostEstimate(
            flops=4 * count * depth * LANES, bytes_accessed=400_000, transcendentals=0
        ),
    )(table, data)


def filter_kernel(first_ref, in_ref, keep_ref, weight_ref, out_ref, given, made, weights, sems):
    first = first_ref[0]
    copies = []
    for degree in range(PER):
        copy = pltpu.make_async_copy(
            weight_ref.at[first + degree], weights.at[degree], sems.at[degree]
        )
        copy.start()
        copies.append(copy)
    kept = jnp.sum(keep_ref[:, COLS : COLS + 1, :].astype(F32), axis=0)
    kept = jnp.broadcast_to(kept, (LANES, LANES)).T
    given[...] = in_ref[...].astype(F32)
    for degree in range(PER):
        lines = [
            jnp.concatenate(
                [
                    given[pl.ds(third * 8 + degree * 2 + part, LAT, stride=THIRDS * 8), :]
                    for third in range(THIRDS)
                ],
                axis=1,
            )
            for part in range(2)
        ]
        lines = jnp.concatenate(lines, axis=0).astype(BF16)
        copies[degree].wait()
        mixed = jnp.dot(lines, weights[degree], preferred_element_type=F32)
        for third in range(THIRDS):
            piece = mixed[:, third * LANES : (third + 1) * LANES]
            piece = piece * kept[degree * 2 * LAT : (degree + 1) * 2 * LAT]
            for part in range(2):
                made[pl.ds(third * 8 + degree * 2 + part, LAT, stride=THIRDS * 8), :] = piece[
                    part * LAT : (part + 1) * LAT
                ]
    out_ref[...] = made[...].astype(BF16)


def filtered(first, data, carried, weight):
    vmem = pl.BlockSpec(memory_space=pltpu.VMEM)
    return pl.pallas_call(
        filter_kernel,
        name="filter",
        out_shape=jax.ShapeDtypeStruct(data.shape, BF16),
        in_specs=[
            pl.BlockSpec(memory_space=pltpu.SMEM), vmem, vmem, pl.BlockSpec(memory_space=pl.ANY)
        ],
        out_specs=vmem,
        scratch_shapes=[
            pltpu.VMEM(data.shape, F32),
            pltpu.VMEM(data.shape, F32),
            pltpu.VMEM((PER, C, C), BF16),
            pltpu.SemaphoreType.DMA((PER,)),
        ],
        cost_estimate=pl.CostEstimate(
            flops=2 * PER * 256 * C * C, bytes_accessed=1_700_000, transcendentals=0
        ),
    )(first[None], data, carried, weight)


def finish_kernel(held_ref, in_ref, out_ref):
    for row in range(ROWS):
        physical = jnp.concatenate([in_ref[lon_of(row, t)] for t in range(THIRDS)], axis=1)
        value = held_ref[row] + gelu(physical.astype(F32))
        out_ref[row] = value[:COLS]


def finished(held, physical):
    vmem = pl.BlockSpec(memory_space=pltpu.VMEM)
    return pl.pallas_call(
        finish_kernel,
        name="finish",
        out_shape=jax.ShapeDtypeStruct((ROWS, COLS, C), F32),
        in_specs=[vmem, vmem],
        out_specs=vmem,
        cost_estimate=pl.CostEstimate(flops=3_000_000, bytes_accessed=800_000, transcendentals=70_000),
    )(held, physical)


def exchange(data, axis, groups=None):
    return lax.all_to_all(data, axis, 0, 0, tiled=True, axis_index_groups=groups)


def by_orders(data):
    data = exchange(data.reshape(LAT * SLOTS, 2, LANES), ("lat", "lon"), ORDER_GROUPS)
    return data.reshape(LAT * SLOTS * 2, LANES)


def by_degrees(data):
    data = exchange(data.reshape(LON, 8, LANES), ("lat", "lon"), DEGREE_GROUPS)
    return data.reshape(LON * 8, LANES)


def by_slots(keep, lon):
    keep = keep.astype(F32).reshape(THIRDS, PER, 1, 1, 4)
    here = (jnp.arange(4) == lon % THIRDS).astype(F32).reshape(1, 1, 1, 4, 1)
    lanes = jnp.broadcast_to(keep * here, (THIRDS, PER, 2, 4, 4)).reshape(THIRDS, 1, LANES)
    slot = (jnp.arange(SLOTS) == lon // THIRDS).astype(F32).reshape(1, SLOTS, 1)
    return lanes * slot


def lon_sums(table, data, dim, factor):
    dims = (((dim,), (0,)), ((), ()))
    return (lax.dot_general(table, data, dims, preferred_element_type=F32) * factor).astype(BF16)


def halo(x):
    up = [(i, i + 1) for i in range(LAT - 1)]
    down = [(j, i) for i, j in up]
    top = lax.ppermute(x[ROWS - 2 :], "lat", up)
    bottom = lax.ppermute(x[:2], "lat", down)
    east = [(i, (i + 1) % LON) for i in range(LON)]
    west = [(j, i) for i, j in east]
    last = jnp.concatenate([top[:, -2:], x[:, -2:], bottom[:, -2:]], axis=0)
    first = jnp.concatenate([top[:, :2], x[:, :2], bottom[:, :2]], axis=0)
    left = lax.ppermute(last, "lon", east)
    right = lax.ppermute(first, "lon", west)
    return top, bottom, left, right


def per_device(grid_state, norm_gain, conv_weight, filter_weight, degree_keep):
    lat, lon = lax.axis_index("lat"), lax.axis_index("lon")
    turn = lon // 2 % 12
    slot, third = lon // 24 * 8 + turn // THIRDS * 2 + lon % 2, turn % THIRDS
    waves = lon_table()
    analysis, synthesis = legendre(jnp.minimum(slot * ROWS + lat, MODES - 1))
    keep = by_slots(degree_keep, lon)
    edges = halo(grid_state)
    held, data = convolutions(lat, grid_state, *edges, keep, norm_gain, conv_weight)
    carried = exchange(data, "lon")
    data = lon_sums(waves, carried.reshape(LON * PAD, LANES), 1, 2.0 * math.pi / NLON)
    data = by_orders(data)
    data = by_degrees(lat_sums("analysis", analysis, data))
    data = by_degrees(filtered(third * PER, data, carried, filter_weight))
    data = by_orders(lat_sums("synthesis", synthesis, data))
    data = exchange(lon_sums(waves, data, 0, 1.0).reshape(LON, PAD, LANES), "lon")
    return finished(held, data)


def solution(mesh):
    in_specs = (P("lat", "lon", None), P(), P(), P("lat", None, None), P("lat", "lon"))
    return jax.shard_map(
        per_device, mesh=mesh, in_specs=in_specs, out_specs=P("lat", "lon", None), check_vma=False
    )
```

time: 199 us -> 194 us (0.975)
  blocking collectives: 128 us -> 105 us
  starting transfers between devices: 27.5 us -> 40.6 us
  waiting for transfers between devices: 13.8 us -> 20.9 us
  matrix products: 3.49 us -> 0.69 us
    all_to_all x6 -> x4, blocking collectives: 128 us -> 105 us  [exchange(): lax.all_to_all(data, axis, 0, 0, tiled=True, axis_index_groups=groups)]
    all_to_all x2, starting transfers between devices: 9.44 us -> 20.4 us  [exchange(): lax.all_to_all(data, axis, 0, 0, tiled=True, axis_index_groups=groups)]
    all_to_all x2, waiting for transfers between devices: 10.4 us -> 20.7 us  [exchange(): lax.all_to_all(data, axis, 0, 0, tiled=True, axis_index_groups=groups)]
    dot_general x4 -> x2, matrix products: 3.49 us -> 0.69 us  [lon_sums(): lax.dot_general(table, data, dims, preferred_element_type=F32) * factor]
    ppermute x1, waiting for transfers between devices: 2.52 us -> 0.01 us  [halo(): bottom = lax.ppermute(x[:2], 'lat', down)]
    ppermute x1, starting transfers between devices: 6.82 us -> 8.93 us  [halo(): right = lax.ppermute(first, 'lon', west)]
  transfers between devices with their start and end apart: 6 -> 6, of which waited for: 4 -> 3; matrix products, arithmetic and copies ran while one was open for 2% -> 2% of each run, Pallas kernels for 1% -> 1%
where the time goes in v2:
time: 194 us; the launch traced here: 193 us
  blocking collectives  105 us (54%)
  starting transfers between devices  40.6 us (21%)
  waiting for transfers between devices  20.9 us (11%)
  Pallas kernels  17.9 us (9%)
  local copies, waits for them, and re-layouts  6.35 us (3%)
    all_to_all x4, blocking collectives, exchange(): lax.all_to_all(data, axis, 0, 0, tiled=True, axis_index_groups=groups)  105 us
    all_to_all x2, waiting for transfers between devices, exchange(): lax.all_to_all(data, axis, 0, 0, tiled=True, axis_index_groups=groups)  20.7 us
    all_to_all x2, starting transfers between devices, exchange(): lax.all_to_all(data, axis, 0, 0, tiled=True, axis_index_groups=groups)  20.4 us
    ppermute x1, starting transfers between devices, halo(): right = lax.ppermute(first, 'lon', west)  8.93 us
    pallas_call x1, Pallas kernels, convolutions(): pl.pallas_call(conv_kernel, name='convolutions', out_shape=[jax.ShapeDtyp...  6.49 us
    ppermute x1, starting transfers between devices, halo(): left = lax.ppermute(last, 'lon', east)  5.36 us
    ppermute x1, starting transfers between devices, halo(): top = lax.ppermute(x[ROWS - 2:], 'lat', up)  4.56 us
  transfers between devices with their start and end apart: 6, of which 3 were waited for; matrix products, arithmetic and copies ran while one was open for 2% of the time, Pallas kernels for 1%

profile of v2, /device:TPU:1, one launch (start us, length us, event | category | flops | bytes accessed | tf_op | source)
XLA Modules:
  0.0 192.9 jit_solution(9685557619699847817)
XLA Ops:
  0.0 0.9 fusion.4
  0.9 1.3 collective-permute-start.1
  2.2 4.6 %collective-permute-start = (f32[2,15,384]{2,1,0:T(8,128)S(1)}, f32[2,15,384]{2,1,0:T(8,128)S(1)}, u32[]{:S(2)}, u32[]{:S(2)}) collective-permute-start(f32[2,15,384]{2,1,0:T(8,128)S(1)} %get-tuple-element.16), channel_id=1, source_target_pairs={{0,48},{48,96},{96,144},{144,192},{192,240},{240,288},{288,336},{3... | collective-permute-start | bytes 138248 | tf_op jit(solution)/shard_map/ppermute | solution.py:371
  6.8 1.0 fusion.3
  7.8 0.7 convert_element_type.29
  9.0 5.4 %collective-permute-start.2 = (f32[16,2,384]{2,1,0:T(2,128)S(1)}, f32[16,2,384]{2,1,0:T(2,128)S(1)}, u32[]{:S(2)}, u32[]{:S(2)}) collective-permute-start(f32[16,2,384]{2,1,0:T(2,128)S(1)} %pad_maximum_fusion), channel_id=1, source_target_pairs={{0,1},{1,2},{2,3},{3,4},{4,5},{5,6},{6,7},{7,8},{8,9},{9,10},{10,1... | collective-permute-start | bytes 147464 | tf_op jit(solution)/shard_map/ppermute | solution.py:377
  14.4 8.9 %collective-permute-start.3 = (f32[16,2,384]{2,1,0:T(2,128)S(1)}, f32[16,2,384]{2,1,0:T(2,128)S(1)}, u32[]{:S(2)}, u32[]{:S(2)}) collective-permute-start(f32[16,2,384]{2,1,0:T(2,128)S(1)} %pad_maximum_fusion.1), channel_id=1, source_target_pairs={{1,0},{2,1},{3,2},{4,3},{5,4},{6,5},{7,6},{8,7},{9,8},{10,9},{11,1... | collective-permute-start | bytes 147464 | tf_op jit(solution)/shard_map/ppermute | solution.py:378
  23.4 0.7 broadcast_multiply_fusion.keep_ref
  24.1 0.2 collective-permute-done.3.right_ref
  24.2 0.4 copy-done.6
  24.7 0.2 copy-done.7
  24.8 6.5 %convolutions.1 = (f32[12,16,384]{2,1,0:T(8,128)}, bf16[48,16,128]{2,1,0:T(8,128)(2,1)}) custom-call(s32[1]{0:T(128)} %bitcast.place_ref, f32[12,15,384]{2,1,0:T(8,128)} %x_ref.1, f32[2,15,384]{2,1,0:T(8,128)} %copy-done.5, f32[2,15,384]{2,1,0:T(8,128)} %copy-done.4, f32[16,2,384]{2,1,0:T(2,128)} %copy-done.6, f32[16,2,384]{2,1,0:T(2,128)} %copy-done.7, ...), custom_call_target="tpu_custom_call" | custom-call | flops 1358954496 | bytes 6500000 | tf_op jit(solution)/shard_map/convolutions/pallas_call | solution.py:211
  31.3 35.8 %all_to_all.30.keep_ref = bf16[48,16,128]{2,1,0:T(8,128)(2,1)S(1)} all-to-all(bf16[48,16,128]{2,1,0:T(8,128)(2,1)} %get-tuple-element.12), channel_id=1, replica_groups=mesh['lat'=16,'lon'=48] {'lon'}, dimensions={0} | all-to-all | bytes 393216 | tf_op jit(solution)/shard_map/all_to_all | solution.py:342
  67.1 0.4 fusion.2
  67.5 0.8 copy.13
  68.3 13.0 %all-to-all-start.1 = ((bf16[256,2,128]{2,1,0:T(2,128)(2,1)}), bf16[256,2,128]{2,1,0:T(2,128)(2,1)S(1)}, u32[]{:S(2)}, u32[]{:S(2)}) async-start(bf16[256,2,128]{2,1,0:T(2,128)(2,1)} %bitcast.6), calls=%async_computation.1 | async-start | bytes 262144 | tf_op jit(solution)/shard_map/all_to_all | solution.py:342
  81.4 1.3 dynamic-slice_bitcast_fusion.coeff_ref.start_ref
  82.7 2.6 %legendre.1 = (bf16[192,256]{1,0:T(8,128)(2,1)}, bf16[256,192]{1,0:T(8,128)(2,1)}) custom-call(s32[1]{0:T(128)} %bitcast.1.order_ref, f32[3,256]{1,0:T(4,128)} %dynamic-slice_bitcast_fusion.coeff_ref.start_ref, f32[3,256]{1,0:T(4,128)} %dynamic-slice_bitcast_fusion.coeff_ref.start_ref, f32[2,256]{1,0:T(2,128)} %constant.80.clone.rows_ref), custom_call_target="tpu_custom_call" | custom-call | flops 6000000 | bytes 300000 | tf_op jit(solution)/shard_map/legendre/pallas_call | solution.py:109
  85.2 12.0 %all-to-all-done.1 = bf16[256,2,128]{2,1,0:T(2,128)(2,1)S(1)} async-done(((bf16[256,2,128]{2,1,0:T(2,128)(2,1)}), bf16[256,2,128]{2,1,0:T(2,128)(2,1)S(1)}, u32[]{:S(2)}, u32[]{:S(2)}) %all-to-all-start.1) | async-done | bytes 131104 | tf_op jit(solution)/shard_map/all_to_all | solution.py:342
  97.2 0.6 copy-done.2
  97.9 1.8 analysis.1
  99.7 7.4 %all-to-all-start.2 = ((bf16[48,8,128]{2,1,0:T(8,128)(2,1)}), bf16[48,8,128]{2,1,0:T(8,128)(2,1)S(1)}, u32[]{:S(2)}, u32[]{:S(2)}) async-start(bf16[48,8,128]{2,1,0:T(8,128)(2,1)} %bitcast.30), calls=%async_computation.2 | async-start | bytes 196608 | tf_op jit(solution)/shard_map/all_to_all | solution.py:342
  107.1 8.7 %all-to-all-done.2 = bf16[48,8,128]{2,1,0:T(8,128)(2,1)S(1)} async-done(((bf16[48,8,128]{2,1,0:T(8,128)(2,1)}), bf16[48,8,128]{2,1,0:T(8,128)(2,1)S(1)}, u32[]{:S(2)}, u32[]{:S(2)}) %all-to-all-start.2) | async-done | bytes 98336 | tf_op jit(solution)/shard_map/all_to_all | solution.py:342
  115.8 0.6 copy-done.3
  116.5 3.3 %filter.1 = bf16[384,128]{1,0:T(8,128)(2,1)} custom-call(s32[1]{0:T(128)} %bitcast.3.first_ref, bf16[384,128]{1,0:T(8,128)(2,1)} %bitcast.32, bf16[48,16,128]{2,1,0:T(8,128)(2,1)} %copy-done.1, bf16[12,384,384]{2,1,0:T(8,128)(2,1)} %weight_ref.3), custom_call_target="tpu_custom_call" | custom-call | flops 301989888 | bytes 1700000 | tf_op jit(solution)/shard_map/filter/pallas_call | solution.py:302
  119.8 14.1 %all_to_all.31 = bf16[48,8,128]{2,1,0:T(8,128)(2,1)} all-to-all(bf16[48,8,128]{2,1,0:T(8,128)(2,1)} %bitcast.33), channel_id=1, replica_groups={{0,2,4,48,50,52,96,98,100,144,146,148,192,194,196,240,242,244,288,290,2..., dimensions={0} | all-to-all | bytes 196608 | tf_op jit(solution)/shard_map/all_to_all | solution.py:342
  133.9 1.9 synthesis.1
  135.8 30.8 %all_to_all.32 = bf16[256,2,128]{2,1,0:T(2,128)(2,1)S(1)} all-to-all(bf16[256,2,128]{2,1,0:T(2,128)(2,1)} %bitcast.29), channel_id=1, replica_groups={{0,1,6,7,12,13,18,19,24,25,30,31,36,37,42,43,48,49,54,55,60,61,66,67,72..., dimensions={0} | all-to-all | bytes 262144 | tf_op jit(solution)/shard_map/all_to_all | solution.py:342
  166.6 0.3 fusion
  166.9 0.2 copy.14
  167.0 24.1 %all_to_all.33.in_ref = bf16[48,16,128]{2,1,0:T(8,128)(2,1)} all-to-all(bf16[48,16,128]{2,1,0:T(8,128)(2,1)S(1)} %bitcast.26), channel_id=1, replica_groups=mesh['lat'=16,'lon'=48] {'lon'}, dimensions={0} | all-to-all | bytes 393216 | tf_op jit(solution)/shard_map/all_to_all | solution.py:342
  191.1 1.8 finish.1
  (26 shorter events, 0.5 us)
Async XLA Ops:
  0.0 67.1 %copy-start = (bf16[512,768]{1,0:T(8,128)(2,1)S(1)}, bf16[512,768]{1,0:T(8,128)(2,1)}, u32[]{:S(2)}) copy-start(bf16[512,768]{1,0:T(8,128)(2,1)} %constant.78.clone) | copy-start | bytes 2359300
  0.9 8.0 %collective-permute-start.1 = (f32[2,15,384]{2,1,0:T(8,128)S(1)}, f32[2,15,384]{2,1,0:T(8,128)S(1)}, u32[]{:S(2)}, u32[]{:S(2)}) collective-permute-start(f32[2,15,384]{2,1,0:T(8,128)S(1)} %get-tuple-element.15), channel_id=1, source_target_pairs={{48,0},{96,48},{144,96},{192,144},{240,192},{288,240},{336,288},{3... | collective-permute-start | bytes 138248 | tf_op jit(solution)/shard_map/ppermute | solution.py:372
  2.2 6.8 %collective-permute-start = (f32[2,15,384]{2,1,0:T(8,128)S(1)}, f32[2,15,384]{2,1,0:T(8,128)S(1)}, u32[]{:S(2)}, u32[]{:S(2)}) collective-permute-start(f32[2,15,384]{2,1,0:T(8,128)S(1)} %get-tuple-element.16), channel_id=1, source_target_pairs={{0,48},{48,96},{96,144},{144,192},{192,240},{240,288},{288,336},{3... | collective-permute-start | bytes 138248 | tf_op jit(solution)/shard_map/ppermute | solution.py:371
  8.9 15.3 %copy-start.4 = (f32[2,15,384]{2,1,0:T(8,128)}, f32[2,15,384]{2,1,0:T(8,128)S(1)}, u32[]{:S(2)}) copy-start(f32[2,15,384]{2,1,0:T(8,128)S(1)} %collective-permute-done.1.bottom_ref) | copy-start | bytes 138244
  9.0 15.3 %copy-start.5 = (f32[2,15,384]{2,1,0:T(8,128)}, f32[2,15,384]{2,1,0:T(8,128)S(1)}, u32[]{:S(2)}) copy-start(f32[2,15,384]{2,1,0:T(8,128)S(1)} %collective-permute-done.top_ref) | copy-start | bytes 138244
  9.0 15.0 %collective-permute-start.2 = (f32[16,2,384]{2,1,0:T(2,128)S(1)}, f32[16,2,384]{2,1,0:T(2,128)S(1)}, u32[]{:S(2)}, u32[]{:S(2)}) collective-permute-start(f32[16,2,384]{2,1,0:T(2,128)S(1)} %pad_maximum_fusion), channel_id=1, source_target_pairs={{0,1},{1,2},{2,3},{3,4},{4,5},{5,6},{6,7},{7,8},{8,9},{9,10},{10,1... | collective-permute-start | bytes 147464 | tf_op jit(solution)/shard_map/ppermute | solution.py:377
  14.4 9.8 %collective-permute-start.3 = (f32[16,2,384]{2,1,0:T(2,128)S(1)}, f32[16,2,384]{2,1,0:T(2,128)S(1)}, u32[]{:S(2)}, u32[]{:S(2)}) collective-permute-start(f32[16,2,384]{2,1,0:T(2,128)S(1)} %pad_maximum_fusion.1), channel_id=1, source_target_pairs={{1,0},{2,1},{3,2},{4,3},{5,4},{6,5},{7,6},{8,7},{9,8},{10,9},{11,1... | collective-permute-start | bytes 147464 | tf_op jit(solution)/shard_map/ppermute | solution.py:378
  24.0 0.6 copy-start.6
  24.2 0.6 copy-start.7
  67.1 48.7 %copy-start.1 = (bf16[48,16,128]{2,1,0:T(8,128)(2,1)}, bf16[48,16,128]{2,1,0:T(8,128)(2,1)S(1)}, u32[]{:S(2)}) copy-start(bf16[48,16,128]{2,1,0:T(8,128)(2,1)S(1)} %all_to_all.30.keep_ref) | copy-start | bytes 589828
  68.3 28.9 %all-to-all-start.1 = ((bf16[256,2,128]{2,1,0:T(2,128)(2,1)}), bf16[256,2,128]{2,1,0:T(2,128)(2,1)S(1)}, u32[]{:S(2)}, u32[]{:S(2)}) async-start(bf16[256,2,128]{2,1,0:T(2,128)(2,1)} %bitcast.6), calls=%async_computation.1 | async-start | bytes 262144 | tf_op jit(solution)/shard_map/all_to_all | solution.py:342
  97.2 0.6 copy-start.2
  99.7 16.2 %all-to-all-start.2 = ((bf16[48,8,128]{2,1,0:T(8,128)(2,1)}), bf16[48,8,128]{2,1,0:T(8,128)(2,1)S(1)}, u32[]{:S(2)}, u32[]{:S(2)}) async-start(bf16[48,8,128]{2,1,0:T(8,128)(2,1)} %bitcast.30), calls=%async_computation.2 | async-start | bytes 196608 | tf_op jit(solution)/shard_map/all_to_all | solution.py:342
  115.8 0.6 copy-start.3

commit v3 on v2

--- a/solution.py
+++ b/solution.py
@@ -74,6 +74,10 @@
     return table.astype(np.float32), np.concatenate([cosine, weight], 0).astype(np.float32)
 
 
+def grant(mebibytes):
+    return pltpu.CompilerParams(vmem_limit_bytes=mebibytes * 2**20)
+
+
 def gelu(value):
     return 0.5 * value * (1.0 + lax.erf(value * math.sqrt(0.5)))
 
@@ -109,6 +113,7 @@
     return pl.pallas_call(
         legendre_kernel,
         name="legendre",
+        compiler_params=grant(6),
         out_shape=[
             jax.ShapeDtypeStruct((MODES, side), BF16),
             jax.ShapeDtypeStruct((side, MODES), BF16),
@@ -251,6 +256,7 @@
     return pl.pallas_call(
         lat_kernel,
         name=name,
+        compiler_params=grant(6),
         out_shape=jax.ShapeDtypeStruct((2 * count, LANES), BF16),
         in_specs=[vmem, vmem],
         out_specs=vmem,
@@ -261,15 +267,8 @@
     )(table, data)
 
 
-def filter_kernel(first_ref, in_ref, keep_ref, weight_ref, out_ref, given, made, weights, sems):
+def filter_kernel(first_ref, in_ref, keep_ref, weight_ref, out_ref, given, made):
     first = first_ref[0]
-    copies = []
-    for degree in range(PER):
-        copy = pltpu.make_async_copy(
-            weight_ref.at[first + degree], weights.at[degree], sems.at[degree]
-        )
-        copy.start()
-        copies.append(copy)
     kept = jnp.sum(keep_ref[:, COLS : COLS + 1, :].astype(F32), axis=0)
     kept = jnp.broadcast_to(kept, (LANES, LANES)).T
     given[...] = in_ref[...].astype(F32)
@@ -285,8 +284,7 @@
             for part in range(2)
         ]
         lines = jnp.concatenate(lines, axis=0).astype(BF16)
-        copies[degree].wait()
-        mixed = jnp.dot(lines, weights[degree], preferred_element_type=F32)
+        mixed = jnp.dot(lines, weight_ref[first + degree], preferred_element_type=F32)
         for third in range(THIRDS):
             piece = mixed[:, third * LANES : (third + 1) * LANES]
             piece = piece * kept[degree * 2 * LAT : (degree + 1) * 2 * LAT]
@@ -302,16 +300,13 @@
     return pl.pallas_call(
         filter_kernel,
         name="filter",
+        compiler_params=grant(8),
         out_shape=jax.ShapeDtypeStruct(data.shape, BF16),
-        in_specs=[
-            pl.BlockSpec(memory_space=pltpu.SMEM), vmem, vmem, pl.BlockSpec(memory_space=pl.ANY)
-        ],
+        in_specs=[pl.BlockSpec(memory_space=pltpu.SMEM), vmem, vmem, vmem],
         out_specs=vmem,
         scratch_shapes=[
             pltpu.VMEM(data.shape, F32),
             pltpu.VMEM(data.shape, F32),
-            pltpu.VMEM((PER, C, C), BF16),
-            pltpu.SemaphoreType.DMA((PER,)),
         ],
         cost_estimate=pl.CostEstimate(
             flops=2 * PER * 256 * C * C, bytes_accessed=1_700_000, transcendentals=0
@@ -331,6 +326,7 @@
     return pl.pallas_call(
         finish_kernel,
         name="finish",
+        compiler_params=grant(6),
         out_shape=jax.ShapeDtypeStruct((ROWS, COLS, C), F32),
         in_specs=[vmem, vmem],
         out_specs=vmem,
@@ -365,18 +361,18 @@
     return (lax.dot_general(table, data, dims, preferred_element_type=F32) * factor).astype(BF16)
 
 
-def halo(x):
+def lat_halo(x):
     up = [(i, i + 1) for i in range(LAT - 1)]
     down = [(j, i) for i, j in up]
-    top = lax.ppermute(x[ROWS - 2 :], "lat", up)
-    bottom = lax.ppermute(x[:2], "lat", down)
+    return lax.ppermute(x[ROWS - 2 :], "lat", up), lax.ppermute(x[:2], "lat", down)
+
+
+def lon_halo(x, top, bottom):
     east = [(i, (i + 1) % LON) for i in range(LON)]
     west = [(j, i) for i, j in east]
     last = jnp.concatenate([top[:, -2:], x[:, -2:], bottom[:, -2:]], axis=0)
     first = jnp.concatenate([top[:, :2], x[:, :2], bottom[:, :2]], axis=0)
-    left = lax.ppermute(last, "lon", east)
-    right = lax.ppermute(first, "lon", west)
-    return top, bottom, left, right
+    return lax.ppermute(last, "lon", east), lax.ppermute(first, "lon", west)
 
 
 def per_device(grid_state, norm_gain, conv_weight, filter_weight, degree_keep):
@@ -386,13 +382,15 @@
     waves = lon_table()
     analysis, synthesis = legendre(jnp.minimum(slot * ROWS + lat, MODES - 1))
     keep = by_slots(degree_keep, lon)
-    edges = halo(grid_state)
+    ready = (*lat_halo(grid_state), keep, analysis, synthesis, third * PER)
+    top, bottom, keep, analysis, synthesis, degree = lax.optimization_barrier(ready)
+    edges = (top, bottom, *lon_halo(grid_state, top, bottom))
     held, data = convolutions(lat, grid_state, *edges, keep, norm_gain, conv_weight)
     carried = exchange(data, "lon")
     data = lon_sums(waves, carried.reshape(LON * PAD, LANES), 1, 2.0 * math.pi / NLON)
     data = by_orders(data)
     data = by_degrees(lat_sums("analysis", analysis, data))
-    data = by_degrees(filtered(third * PER, data, carried, filter_weight))
+    data = by_degrees(filtered(degree, data, carried, filter_weight))
     data = by_orders(lat_sums("synthesis", synthesis, data))
     data = exchange(lon_sums(waves, data, 0, 1.0).reshape(LON, PAD, LANES), "lon")
     return finished(held, data)

time: 194 us -> 203 us (1.046)
  blocking collectives: 105 us -> 147 us
  waiting for transfers between devices: 20.9 us -> 0.99 us
  starting transfers between devices: 40.6 us -> 20.8 us
  local copies, waits for them, and re-layouts: 6.35 us -> 14.6 us
  Pallas kernels: 17.9 us -> 9.83 us
  other arithmetic: 1.49 us -> 5.31 us
  matrix products: 0.69 us -> 3.6 us
    all_to_all x4 -> x6, blocking collectives: 105 us -> 147 us  [exchange(): lax.all_to_all(data, axis, 0, 0, tiled=True, axis_index_groups=groups)]
    all_to_all x2 -> x0, waiting for transfers between devices: 20.7 us -> none  [exchange(): lax.all_to_all(data, axis, 0, 0, tiled=True, axis_index_groups=groups)]
    all_to_all x2 -> x0, starting transfers between devices: 20.4 us -> none  [exchange(): lax.all_to_all(data, axis, 0, 0, tiled=True, axis_index_groups=groups)]
    pallas_call x5, Pallas kernels: 11.4 us -> 3.34 us  [the longest x1 1.79 us: legendre(): pl.pallas_call(legendre_kernel, name='legendre', compiler_params=grant(6)...]
    unnamed x16 -> x18, local copies, waits for them, and re-layouts: 1.9 us -> 6.31 us
    dot_general x2, matrix products: 0.69 us -> 3.6 us  [lon_sums(): lax.dot_general(table, data, dims, preferred_element_type=F32) * factor]
    slice x4 -> x3, local copies, waits for them, and re-layouts: 1.93 us -> 4.04 us  [the longest x2 2.44 us: lon_halo(): first = jnp.concatenate([top[:, :2], x[:, :2], bottom[:, :2]], axis=0)]
  transfers between devices with their start and end apart: 6 -> 4, of which waited for: 3 -> 1; matrix products, arithmetic and copies ran while one was open for 2% -> 4% of each run, Pallas kernels for 1% -> 1%
where the time goes in v3:
time: 203 us; the launch traced here: 202 us
  blocking collectives  147 us (72%)
  starting transfers between devices  20.8 us (10%)
  local copies, waits for them, and re-layouts  14.6 us (7%)
  Pallas kernels  9.83 us (5%)
  other arithmetic  5.31 us (3%)
  matrix products  3.6 us (2%)
    all_to_all x6, blocking collectives, exchange(): lax.all_to_all(data, axis, 0, 0, tiled=True, axis_index_groups=groups)  147 us
    ppermute x2, starting transfers between devices, lon_halo(): return (lax.ppermute(last, 'lon', east), lax.ppermute(first, 'lon', west))  14.3 us
    pallas_call x1, Pallas kernels, convolutions(): pl.pallas_call(conv_kernel, name='convolutions', out_shape=[jax.ShapeDtyp...  6.49 us
    unnamed x18, local copies, waits for them, and re-layouts  6.31 us
    ppermute x1, starting transfers between devices, lat_halo(): lax.ppermute(x[ROWS - 2:], 'lat', up)  5.18 us
  transfers between devices with their start and end apart: 4, of which 1 were waited for; matrix products, arithmetic and copies ran while one was open for 4% of the time, Pallas kernels for 1%

profile of v3, /device:TPU:1, one launch (start us, length us, event | category | flops | bytes accessed | tf_op | source)
XLA Modules:
  0.0 202.0 jit_solution(10206749668123533344)
XLA Ops:
  0.0 1.6 fusion.4
  1.6 1.3 collective-permute-start.1
  2.9 5.2 %collective-permute-start = (f32[2,15,384]{2,1,0:T(8,128)}, f32[2,15,384]{2,1,0:T(8,128)}, u32[]{:S(2)}, u32[]{:S(2)}) collective-permute-start(f32[2,15,384]{2,1,0:T(8,128)} %get-tuple-element.28), channel_id=1, source_target_pairs={{0,48},{48,96},{96,144},{144,192},{192,240},{240,288},{288,336},{3... | collective-permute-start | bytes 138248 | tf_op jit(solution)/shard_map/ppermute | solution.py:367
  8.1 1.6 fusion.3
  10.8 0.7 convert_element_type.29
  12.9 0.9 mul.58
  13.8 1.3 broadcast_multiply_fusion.keep_ref
  15.2 0.7 dynamic-slice_bitcast_fusion.coeff_ref.start_ref
  15.9 0.7 copy-done.8
  16.5 1.8 legendre.1
  19.6 0.8 fusion.5
  20.4 0.8 pad_maximum_fusion
  21.2 5.4 %collective-permute-start.2 = (f32[16,2,384]{2,1,0:T(2,128)S(1)}, f32[16,2,384]{2,1,0:T(2,128)}, u32[]{:S(2)}, u32[]{:S(2)}) collective-permute-start(f32[16,2,384]{2,1,0:T(2,128)S(1)} %pad_maximum_fusion), channel_id=1, source_target_pairs={{0,1},{1,2},{2,3},{3,4},{4,5},{5,6},{6,7},{7,8},{8,9},{9,10},{10,1... | collective-permute-start | bytes 147464 | tf_op jit(solution)/shard_map/ppermute | solution.py:375
  26.6 0.8 pad_maximum_fusion.1
  27.4 8.9 %collective-permute-start.3 = (f32[16,2,384]{2,1,0:T(2,128)S(1)}, f32[16,2,384]{2,1,0:T(2,128)}, u32[]{:S(2)}, u32[]{:S(2)}) collective-permute-start(f32[16,2,384]{2,1,0:T(2,128)S(1)} %pad_maximum_fusion.1), channel_id=1, source_target_pairs={{1,0},{2,1},{3,2},{4,3},{5,4},{6,5},{7,6},{8,7},{9,8},{10,9},{11,1... | collective-permute-start | bytes 147464 | tf_op jit(solution)/shard_map/ppermute | solution.py:375
  36.3 1.0 collective-permute-done.3.right_ref
  37.3 6.5 %convolutions.1 = (f32[12,16,384]{2,1,0:T(8,128)}, bf16[48,16,128]{2,1,0:T(8,128)(2,1)}) custom-call(s32[1]{0:T(128)} %bitcast.place_ref, f32[12,15,384]{2,1,0:T(8,128)} %x_ref.1, f32[2,15,384]{2,1,0:T(8,128)} %collective-permute-done.top_ref, f32[2,15,384]{2,1,0:T(8,128)} %collective-permute-done.1.bottom_ref, ...), custom_call_target="tpu_custom_call" | custom-call | flops 1358954496 | bytes 6500000 | tf_op jit(solution)/shard_map/convolutions/pallas_call | solution.py:216
  43.8 36.1 %all_to_all.30.keep_ref = bf16[48,16,128]{2,1,0:T(8,128)(2,1)S(1)} all-to-all(bf16[48,16,128]{2,1,0:T(8,128)(2,1)} %get-tuple-element.24), channel_id=1, replica_groups=mesh['lat'=16,'lon'=48] {'lon'}, dimensions={0} | all-to-all | bytes 393216 | tf_op jit(solution)/shard_map/all_to_all | solution.py:338
  79.9 2.2 %fusion.2 = bf16[512,128]{0,1:T(8,128)(2,1)} fusion(bf16[768,128]{1,0:T(8,128)(2,1)S(1)} %bitcast.25, bf16[512,768]{1,0:T(8,128)(2,1)} %constant.78.clone), kind=kOutput, calls=%fused_computation.4 | convolution fusion | flops 100794368 | bytes 1114112 | tf_op jit(solution)/shard_map/dot_general | solution.py:361
  82.1 0.7 copy-done.1
  82.8 1.6 copy.13
  84.4 27.6 %all_to_all.31 = bf16[256,2,128]{2,1,0:T(2,128)(2,1)S(1)} all-to-all(bf16[256,2,128]{2,1,0:T(2,128)(2,1)} %bitcast.34), channel_id=1, replica_groups={{0,1,6,7,12,13,18,19,24,25,30,31,36,37,42,43,48,49,54,55,60,61,66,67,72..., dimensions={0} | all-to-all | bytes 262144 | tf_op jit(solution)/shard_map/all_to_all | solution.py:338
  112.0 0.9 copy-done.7
  113.1 15.9 %all_to_all.32 = bf16[48,8,128]{2,1,0:T(8,128)(2,1)S(1)} all-to-all(bf16[48,8,128]{2,1,0:T(8,128)(2,1)S(1)} %bitcast.28), channel_id=1, replica_groups={{0,2,4,48,50,52,96,98,100,144,146,148,192,194,196,240,242,244,288,290,2..., dimensions={0} | all-to-all | bytes 196608 | tf_op jit(solution)/shard_map/all_to_all | solution.py:338
  129.0 0.9 copy-done.2
  130.3 12.5 %all_to_all.33 = bf16[48,8,128]{2,1,0:T(8,128)(2,1)S(1)} all-to-all(bf16[48,8,128]{2,1,0:T(8,128)(2,1)S(1)} %bitcast.31), channel_id=1, replica_groups={{0,2,4,48,50,52,96,98,100,144,146,148,192,194,196,240,242,244,288,290,2..., dimensions={0} | all-to-all | bytes 196608 | tf_op jit(solution)/shard_map/all_to_all | solution.py:338
  142.7 0.9 copy-done.5
  143.9 30.8 %all_to_all.34 = bf16[256,2,128]{2,1,0:T(2,128)(2,1)S(1)} all-to-all(bf16[256,2,128]{2,1,0:T(2,128)(2,1)S(1)} %bitcast.27), channel_id=1, replica_groups={{0,1,6,7,12,13,18,19,24,25,30,31,36,37,42,43,48,49,54,55,60,61,66,67,72..., dimensions={0} | all-to-all | bytes 262144 | tf_op jit(solution)/shard_map/all_to_all | solution.py:338
  174.7 1.4 fusion
  176.3 24.0 %all_to_all.35.in_ref = bf16[48,16,128]{2,1,0:T(8,128)(2,1)S(1)} all-to-all(bf16[48,16,128]{2,1,0:T(8,128)(2,1)S(1)} %bitcast.32), channel_id=1, replica_groups=mesh['lat'=16,'lon'=48] {'lon'}, dimensions={0} | all-to-all | bytes 393216 | tf_op jit(solution)/shard_map/all_to_all | solution.py:338
  200.2 1.0 copy-done.3
  201.2 0.8 finish.1
  (25 shorter events, 4.7 us)
Async XLA Ops:
  0.0 129.0 %copy-start = (bf16[12,384,384]{2,1,0:T(8,128)(2,1)S(1)}, bf16[12,384,384]{2,1,0:T(8,128)(2,1)}, u32[]{:S(2)}) copy-start(bf16[12,384,384]{2,1,0:T(8,128)(2,1)} %weight_ref.3) | copy-start | bytes 10616836
  1.6 18.0 %collective-permute-start.1 = (f32[2,15,384]{2,1,0:T(8,128)}, f32[2,15,384]{2,1,0:T(8,128)}, u32[]{:S(2)}, u32[]{:S(2)}) collective-permute-start(f32[2,15,384]{2,1,0:T(8,128)} %get-tuple-element.27), channel_id=1, source_target_pairs={{48,0},{96,48},{144,96},{192,144},{240,192},{288,240},{336,288},{3... | collective-permute-start | bytes 138248 | tf_op jit(solution)/shard_map/ppermute | solution.py:367
  2.9 16.7 %collective-permute-start = (f32[2,15,384]{2,1,0:T(8,128)}, f32[2,15,384]{2,1,0:T(8,128)}, u32[]{:S(2)}, u32[]{:S(2)}) collective-permute-start(f32[2,15,384]{2,1,0:T(8,128)} %get-tuple-element.28), channel_id=1, source_target_pairs={{0,48},{48,96},{96,144},{144,192},{192,240},{240,288},{288,336},{3... | collective-permute-start | bytes 138248 | tf_op jit(solution)/shard_map/ppermute | solution.py:367
  15.9 0.7 copy-start.8
  18.3 0.7 copy-start.4
  19.0 0.6 copy-start.6
  21.2 15.1 %collective-permute-start.2 = (f32[16,2,384]{2,1,0:T(2,128)S(1)}, f32[16,2,384]{2,1,0:T(2,128)}, u32[]{:S(2)}, u32[]{:S(2)}) collective-permute-start(f32[16,2,384]{2,1,0:T(2,128)S(1)} %pad_maximum_fusion), channel_id=1, source_target_pairs={{0,1},{1,2},{2,3},{3,4},{4,5},{5,6},{6,7},{7,8},{8,9},{9,10},{10,1... | collective-permute-start | bytes 147464 | tf_op jit(solution)/shard_map/ppermute | solution.py:375
  27.4 9.9 %collective-permute-start.3 = (f32[16,2,384]{2,1,0:T(2,128)S(1)}, f32[16,2,384]{2,1,0:T(2,128)}, u32[]{:S(2)}, u32[]{:S(2)}) collective-permute-start(f32[16,2,384]{2,1,0:T(2,128)S(1)} %pad_maximum_fusion.1), channel_id=1, source_target_pairs={{1,0},{2,1},{3,2},{4,3},{5,4},{6,5},{7,6},{8,7},{9,8},{10,9},{11,1... | collective-permute-start | bytes 147464 | tf_op jit(solution)/shard_map/ppermute | solution.py:375
  82.1 0.7 copy-start.1
  112.0 0.9 copy-start.7
  129.0 0.9 copy-start.2
  142.7 0.9 copy-start.5
  200.2 1.0 copy-start.3

commit v4 on v2

--- a/solution.py
+++ b/solution.py
@@ -74,6 +74,10 @@
     return table.astype(np.float32), np.concatenate([cosine, weight], 0).astype(np.float32)
 
 
+def grant(mebibytes):
+    return pltpu.CompilerParams(vmem_limit_bytes=mebibytes * 2**20)
+
+
 def gelu(value):
     return 0.5 * value * (1.0 + lax.erf(value * math.sqrt(0.5)))
 
@@ -109,6 +113,7 @@
     return pl.pallas_call(
         legendre_kernel,
         name="legendre",
+        compiler_params=grant(6),
         out_shape=[
             jax.ShapeDtypeStruct((MODES, side), BF16),
             jax.ShapeDtypeStruct((side, MODES), BF16),
@@ -251,6 +256,7 @@
     return pl.pallas_call(
         lat_kernel,
         name=name,
+        compiler_params=grant(6),
         out_shape=jax.ShapeDtypeStruct((2 * count, LANES), BF16),
         in_specs=[vmem, vmem],
         out_specs=vmem,
@@ -302,6 +308,7 @@
     return pl.pallas_call(
         filter_kernel,
         name="filter",
+        compiler_params=grant(61),
         out_shape=jax.ShapeDtypeStruct(data.shape, BF16),
         in_specs=[
             pl.BlockSpec(memory_space=pltpu.SMEM), vmem, vmem, pl.BlockSpec(memory_space=pl.ANY)
@@ -331,6 +338,7 @@
     return pl.pallas_call(
         finish_kernel,
         name="finish",
+        compiler_params=grant(6),
         out_shape=jax.ShapeDtypeStruct((ROWS, COLS, C), F32),
         in_specs=[vmem, vmem],
         out_specs=vmem,
@@ -365,18 +373,18 @@
     return (lax.dot_general(table, data, dims, preferred_element_type=F32) * factor).astype(BF16)
 
 
-def halo(x):
+def lat_halo(x):
     up = [(i, i + 1) for i in range(LAT - 1)]
     down = [(j, i) for i, j in up]
-    top = lax.ppermute(x[ROWS - 2 :], "lat", up)
-    bottom = lax.ppermute(x[:2], "lat", down)
+    return lax.ppermute(x[ROWS - 2 :], "lat", up), lax.ppermute(x[:2], "lat", down)
+
+
+def lon_halo(x, top, bottom):
     east = [(i, (i + 1) % LON) for i in range(LON)]
     west = [(j, i) for i, j in east]
     last = jnp.concatenate([top[:, -2:], x[:, -2:], bottom[:, -2:]], axis=0)
     first = jnp.concatenate([top[:, :2], x[:, :2], bottom[:, :2]], axis=0)
-    left = lax.ppermute(last, "lon", east)
-    right = lax.ppermute(first, "lon", west)
-    return top, bottom, left, right
+    return lax.ppermute(last, "lon", east), lax.ppermute(first, "lon", west)
 
 
 def per_device(grid_state, norm_gain, conv_weight, filter_weight, degree_keep):
@@ -386,13 +394,15 @@
     waves = lon_table()
     analysis, synthesis = legendre(jnp.minimum(slot * ROWS + lat, MODES - 1))
     keep = by_slots(degree_keep, lon)
-    edges = halo(grid_state)
+    top, bottom = lat_halo(grid_state)
+    top, bottom, degree = lax.optimization_barrier((top, bottom, third * PER))
+    edges = (top, bottom, *lon_halo(grid_state, top, bottom))
     held, data = convolutions(lat, grid_state, *edges, keep, norm_gain, conv_weight)
     carried = exchange(data, "lon")
     data = lon_sums(waves, carried.reshape(LON * PAD, LANES), 1, 2.0 * math.pi / NLON)
     data = by_orders(data)
     data = by_degrees(lat_sums("analysis", analysis, data))
-    data = by_degrees(filtered(third * PER, data, carried, filter_weight))
+    data = by_degrees(filtered(degree, data, carried, filter_weight))
     data = by_orders(lat_sums("synthesis", synthesis, data))
     data = exchange(lon_sums(waves, data, 0, 1.0).reshape(LON, PAD, LANES), "lon")
     return finished(held, data)

time: 194 us -> 189 us (0.974)
  starting transfers between devices: 40.6 us -> 29.5 us
  blocking collectives: 105 us -> 115 us
  Pallas kernels: 17.9 us -> 12.9 us
  waiting for transfers between devices: 20.9 us -> 23.8 us
    all_to_all x4 -> x5, blocking collectives: 105 us -> 115 us  [exchange(): lax.all_to_all(data, axis, 0, 0, tiled=True, axis_index_groups=groups)]
    ppermute x4, waiting for transfers between devices: 0.19 us -> 10.4 us  [the longest x2 9.09 us: lon_halo(): return (lax.ppermute(last, 'lon', east), lax.ppermute(first, 'lon', west))]
    all_to_all x2 -> x1, starting transfers between devices: 20.4 us -> 11.5 us  [exchange(): lax.all_to_all(data, axis, 0, 0, tiled=True, axis_index_groups=groups)]
    all_to_all x2 -> x1, waiting for transfers between devices: 20.7 us -> 13.3 us  [exchange(): lax.all_to_all(data, axis, 0, 0, tiled=True, axis_index_groups=groups)]
    pallas_call x5, Pallas kernels: 11.4 us -> 6.37 us  [the longest x1 3.33 us: filtered(): pl.pallas_call(filter_kernel, name='filter', compiler_params=grant(61), o...]
    ppermute x4, starting transfers between devices: 20.1 us -> 18 us  [the longest x2 12.8 us: lon_halo(): return (lax.ppermute(last, 'lon', east), lax.ppermute(first, 'lon', west))]
  transfers between devices with their start and end apart: 6 -> 5, of which waited for: 3 -> 3; matrix products, arithmetic and copies ran while one was open for 2% -> 2% of each run, Pallas kernels for 1% -> 1%
where the time goes in v4:
time: 189 us
  blocking collectives  115 us (61%)
  starting transfers between devices  29.5 us (16%)
  waiting for transfers between devices  23.8 us (13%)
  Pallas kernels  12.9 us (7%)
  local copies, waits for them, and re-layouts  4.49 us (2%)
    all_to_all x5, blocking collectives, exchange(): lax.all_to_all(data, axis, 0, 0, tiled=True, axis_index_groups=groups)  115 us
    all_to_all x1, waiting for transfers between devices, exchange(): lax.all_to_all(data, axis, 0, 0, tiled=True, axis_index_groups=groups)  13.3 us
    ppermute x2, starting transfers between devices, lon_halo(): return (lax.ppermute(last, 'lon', east), lax.ppermute(first, 'lon', west))  12.8 us
    all_to_all x1, starting transfers between devices, exchange(): lax.all_to_all(data, axis, 0, 0, tiled=True, axis_index_groups=groups)  11.5 us
    ppermute x2, waiting for transfers between devices, lon_halo(): return (lax.ppermute(last, 'lon', east), lax.ppermute(first, 'lon', west))  9.09 us
    pallas_call x1, Pallas kernels, convolutions(): pl.pallas_call(conv_kernel, name='convolutions', out_shape=[jax.ShapeDtyp...  6.5 us
    ppermute x1, starting transfers between devices, lat_halo(): lax.ppermute(x[ROWS - 2:], 'lat', up)  3.92 us
  transfers between devices with their start and end apart: 5, of which 3 were waited for; matrix products, arithmetic and copies ran while one was open for 2% of the time, Pallas kernels for 1%

profile of v4, /device:TPU:1, one launch (start us, length us, event | category | flops | bytes accessed | tf_op | source)
XLA Modules:
  0.0 188.5 jit_solution(13318759331916447886)
XLA Ops:
  0.0 0.9 fusion.4
  0.9 3.9 %collective-permute-start = (f32[2,15,384]{2,1,0:T(8,128)S(1)}, f32[2,15,384]{2,1,0:T(8,128)S(1)}, u32[]{:S(2)}, u32[]{:S(2)}) collective-permute-start(f32[2,15,384]{2,1,0:T(8,128)S(1)} %get-tuple-element.22), channel_id=1, source_target_pairs={{0,48},{48,96},{96,144},{144,192},{192,240},{240,288},{288,336},{3... | collective-permute-start | bytes 138248 | tf_op jit(solution)/shard_map/ppermute | solution.py:379
  4.8 1.3 collective-permute-start.1
  6.1 1.0 fusion.3
  7.2 0.7 convert_element_type.29
  7.9 0.1 mul.55
  8.0 0.1 copy.12
  8.2 0.1 mul.59
  8.3 1.3 collective-permute-done.1.bottom_ref
  9.7 10.9 %collective-permute-start.3 = (f32[16,2,384]{2,1,0:T(2,128)S(1)}, f32[16,2,384]{2,1,0:T(2,128)S(1)}, u32[]{:S(2)}, u32[]{:S(2)}) collective-permute-start(f32[16,2,384]{2,1,0:T(2,128)S(1)} %pad_maximum_fusion.1), channel_id=1, source_target_pairs={{1,0},{2,1},{3,2},{4,3},{5,4},{6,5},{7,6},{8,7},{9,8},{10,9},{11,1... | collective-permute-start | bytes 147464 | tf_op jit(solution)/shard_map/ppermute | solution.py:387
  20.7 1.9 %collective-permute-start.2 = (f32[16,2,384]{2,1,0:T(2,128)S(1)}, f32[16,2,384]{2,1,0:T(2,128)S(1)}, u32[]{:S(2)}, u32[]{:S(2)}) collective-permute-start(f32[16,2,384]{2,1,0:T(2,128)S(1)} %pad_maximum_fusion), channel_id=1, source_target_pairs={{0,1},{1,2},{2,3},{3,4},{4,5},{5,6},{6,7},{7,8},{8,9},{9,10},{10,1... | collective-permute-start | bytes 147464 | tf_op jit(solution)/shard_map/ppermute | solution.py:387
  22.6 0.7 broadcast_multiply_fusion.keep_ref
  23.3 9.1 %collective-permute-done.2.left_ref = f32[16,2,384]{2,1,0:T(2,128)S(1)} collective-permute-done((f32[16,2,384]{2,1,0:T(2,128)S(1)}, f32[16,2,384]{2,1,0:T(2,128)S(1)}, u32[]{:S(2)}, u32[]{:S(2)}) %collective-permute-start.2) | collective-permute-done | bytes 49184 | tf_op jit(solution)/shard_map/ppermute | solution.py:387
  32.4 0.6 copy-done.7
  33.0 6.5 %convolutions.1 = (f32[12,16,384]{2,1,0:T(8,128)}, bf16[48,16,128]{2,1,0:T(8,128)(2,1)}) custom-call(s32[1]{0:T(128)} %bitcast.place_ref, f32[12,15,384]{2,1,0:T(8,128)} %x_ref.1, f32[2,15,384]{2,1,0:T(8,128)} %copy-done.4, f32[2,15,384]{2,1,0:T(8,128)} %copy-done.5, f32[16,2,384]{2,1,0:T(2,128)} %copy-done.7, f32[16,2,384]{2,1,0:T(2,128)} %copy-done.6, ...), custom_call_target="tpu_custom_call" | custom-call | flops 1358954496 | bytes 6500000 | tf_op jit(solution)/shard_map/convolutions/pallas_call | solution.py:216
  39.5 31.3 %all_to_all.30.keep_ref = bf16[48,16,128]{2,1,0:T(8,128)(2,1)S(1)} all-to-all(bf16[48,16,128]{2,1,0:T(8,128)(2,1)} %get-tuple-element.18), channel_id=1, replica_groups=mesh['lat'=16,'lon'=48] {'lon'}, dimensions={0} | all-to-all | bytes 393216 | tf_op jit(solution)/shard_map/all_to_all | solution.py:350
  70.8 0.4 fusion.2
  71.2 0.8 copy.13
  71.9 11.5 %all-to-all-start.1 = ((bf16[256,2,128]{2,1,0:T(2,128)(2,1)}), bf16[256,2,128]{2,1,0:T(2,128)(2,1)S(1)}, u32[]{:S(2)}, u32[]{:S(2)}) async-start(bf16[256,2,128]{2,1,0:T(2,128)(2,1)} %bitcast.6), calls=%async_computation.1 | async-start | bytes 262144 | tf_op jit(solution)/shard_map/all_to_all | solution.py:350
  83.5 0.7 dynamic-slice_bitcast_fusion.coeff_ref.start_ref
  84.2 1.8 legendre.1
  86.0 13.3 %all-to-all-done.1 = bf16[256,2,128]{2,1,0:T(2,128)(2,1)S(1)} async-done(((bf16[256,2,128]{2,1,0:T(2,128)(2,1)}), bf16[256,2,128]{2,1,0:T(2,128)(2,1)S(1)}, u32[]{:S(2)}, u32[]{:S(2)}) %all-to-all-start.1) | async-done | bytes 131104 | tf_op jit(solution)/shard_map/all_to_all | solution.py:350
  99.3 0.2 analysis.1
  99.5 16.0 %all_to_all.31 = bf16[48,8,128]{2,1,0:T(8,128)(2,1)} all-to-all(bf16[48,8,128]{2,1,0:T(8,128)(2,1)S(1)} %bitcast.28), channel_id=1, replica_groups={{0,2,4,48,50,52,96,98,100,144,146,148,192,194,196,240,242,244,288,290,2..., dimensions={0} | all-to-all | bytes 196608 | tf_op jit(solution)/shard_map/all_to_all | solution.py:350
  115.6 3.3 %filter.1 = bf16[384,128]{1,0:T(8,128)(2,1)} custom-call(s32[1]{0:T(128)} %bitcast.3.first_ref, bf16[384,128]{1,0:T(8,128)(2,1)} %bitcast.32, bf16[48,16,128]{2,1,0:T(8,128)(2,1)} %copy-done.3, bf16[12,384,384]{2,1,0:T(8,128)(2,1)} %weight_ref.3), custom_call_target="tpu_custom_call" | custom-call | flops 301989888 | bytes 1700000 | tf_op jit(solution)/shard_map/filter/pallas_call | solution.py:308
  118.9 13.4 %all_to_all.32 = bf16[48,8,128]{2,1,0:T(8,128)(2,1)S(1)} all-to-all(bf16[48,8,128]{2,1,0:T(8,128)(2,1)} %bitcast.33), channel_id=1, replica_groups={{0,2,4,48,50,52,96,98,100,144,146,148,192,194,196,240,242,244,288,290,2..., dimensions={0} | all-to-all | bytes 196608 | tf_op jit(solution)/shard_map/all_to_all | solution.py:350
  132.2 0.2 synthesis.1
  132.5 30.8 %all_to_all.33 = bf16[256,2,128]{2,1,0:T(2,128)(2,1)S(1)} all-to-all(bf16[256,2,128]{2,1,0:T(2,128)(2,1)S(1)} %bitcast.26), channel_id=1, replica_groups={{0,1,6,7,12,13,18,19,24,25,30,31,36,37,42,43,48,49,54,55,60,61,66,67,72..., dimensions={0} | all-to-all | bytes 262144 | tf_op jit(solution)/shard_map/all_to_all | solution.py:350
  163.3 0.3 fusion
  163.6 0.2 copy.14
  163.7 24.0 %all_to_all.34.in_ref = bf16[48,16,128]{2,1,0:T(8,128)(2,1)S(1)} all-to-all(bf16[48,16,128]{2,1,0:T(8,128)(2,1)S(1)} %bitcast.30), channel_id=1, replica_groups=mesh['lat'=16,'lon'=48] {'lon'}, dimensions={0} | all-to-all | bytes 393216 | tf_op jit(solution)/shard_map/all_to_all | solution.py:350
  187.7 0.8 finish.1
  (24 shorter events, 0.2 us)
Async XLA Ops:
  0.0 70.8 %copy-start.2 = (bf16[512,768]{1,0:T(8,128)(2,1)S(1)}, bf16[512,768]{1,0:T(8,128)(2,1)}, u32[]{:S(2)}) copy-start(bf16[512,768]{1,0:T(8,128)(2,1)} %constant.78.clone) | copy-start | bytes 2359300
  0.0 84.2 %copy-start.1 = (f32[2,256]{1,0:T(2,128)S(1)}, f32[2,256]{1,0:T(2,128)}, u32[]{:S(2)}) copy-start(f32[2,256]{1,0:T(2,128)} %constant.80.clone.rows_ref) | copy-start | bytes 6148
  0.9 7.4 %collective-permute-start = (f32[2,15,384]{2,1,0:T(8,128)S(1)}, f32[2,15,384]{2,1,0:T(8,128)S(1)}, u32[]{:S(2)}, u32[]{:S(2)}) collective-permute-start(f32[2,15,384]{2,1,0:T(8,128)S(1)} %get-tuple-element.22), channel_id=1, source_target_pairs={{0,48},{48,96},{96,144},{144,192},{192,240},{240,288},{288,336},{3... | collective-permute-start | bytes 138248 | tf_op jit(solution)/shard_map/ppermute | solution.py:379
  4.8 4.8 %collective-permute-start.1 = (f32[2,15,384]{2,1,0:T(8,128)S(1)}, f32[2,15,384]{2,1,0:T(8,128)S(1)}, u32[]{:S(2)}, u32[]{:S(2)}) collective-permute-start(f32[2,15,384]{2,1,0:T(8,128)S(1)} %get-tuple-element.21), channel_id=1, source_target_pairs={{48,0},{96,48},{144,96},{192,144},{240,192},{288,240},{336,288},{3... | collective-permute-start | bytes 138248 | tf_op jit(solution)/shard_map/ppermute | solution.py:379
  8.3 24.0 %copy-start.4 = (f32[2,15,384]{2,1,0:T(8,128)}, f32[2,15,384]{2,1,0:T(8,128)S(1)}, u32[]{:S(2)}) copy-start(f32[2,15,384]{2,1,0:T(8,128)S(1)} %collective-permute-done.top_ref) | copy-start | bytes 138244
  9.7 22.7 %copy-start.5 = (f32[2,15,384]{2,1,0:T(8,128)}, f32[2,15,384]{2,1,0:T(8,128)S(1)}, u32[]{:S(2)}) copy-start(f32[2,15,384]{2,1,0:T(8,128)S(1)} %collective-permute-done.1.bottom_ref) | copy-start | bytes 138244
  9.7 13.5 %collective-permute-start.3 = (f32[16,2,384]{2,1,0:T(2,128)S(1)}, f32[16,2,384]{2,1,0:T(2,128)S(1)}, u32[]{:S(2)}, u32[]{:S(2)}) collective-permute-start(f32[16,2,384]{2,1,0:T(2,128)S(1)} %pad_maximum_fusion.1), channel_id=1, source_target_pairs={{1,0},{2,1},{3,2},{4,3},{5,4},{6,5},{7,6},{8,7},{9,8},{10,9},{11,1... | collective-permute-start | bytes 147464 | tf_op jit(solution)/shard_map/ppermute | solution.py:387
  20.7 11.7 %collective-permute-start.2 = (f32[16,2,384]{2,1,0:T(2,128)S(1)}, f32[16,2,384]{2,1,0:T(2,128)S(1)}, u32[]{:S(2)}, u32[]{:S(2)}) collective-permute-start(f32[16,2,384]{2,1,0:T(2,128)S(1)} %pad_maximum_fusion), channel_id=1, source_target_pairs={{0,1},{1,2},{2,3},{3,4},{4,5},{5,6},{6,7},{7,8},{8,9},{9,10},{10,1... | collective-permute-start | bytes 147464 | tf_op jit(solution)/shard_map/ppermute | solution.py:387
  23.3 9.1 %copy-start.6 = (f32[16,2,384]{2,1,0:T(2,128)}, f32[16,2,384]{2,1,0:T(2,128)S(1)}, u32[]{:S(2)}) copy-start(f32[16,2,384]{2,1,0:T(2,128)S(1)} %collective-permute-done.3.right_ref) | copy-start | bytes 147460
  32.4 0.6 copy-start.7
  39.5 148.2 %copy-start = (f32[12,16,384]{2,1,0:T(8,128)S(1)}, f32[12,16,384]{2,1,0:T(8,128)}, u32[]{:S(2)}) copy-start(f32[12,16,384]{2,1,0:T(8,128)} %get-tuple-element.14.held_ref) | copy-start | bytes 884740
  70.8 44.8 %copy-start.3 = (bf16[48,16,128]{2,1,0:T(8,128)(2,1)}, bf16[48,16,128]{2,1,0:T(8,128)(2,1)S(1)}, u32[]{:S(2)}) copy-start(bf16[48,16,128]{2,1,0:T(8,128)(2,1)S(1)} %all_to_all.30.keep_ref) | copy-start | bytes 589828
  71.9 27.4 %all-to-all-start.1 = ((bf16[256,2,128]{2,1,0:T(2,128)(2,1)}), bf16[256,2,128]{2,1,0:T(2,128)(2,1)S(1)}, u32[]{:S(2)}, u32[]{:S(2)}) async-start(bf16[256,2,128]{2,1,0:T(2,128)(2,1)} %bitcast.6), calls=%async_computation.1 | async-start | bytes 262144 | tf_op jit(solution)/shard_map/all_to_all | solution.py:350

commit v5 on v4

--- a/solution.py
+++ b/solution.py
@@ -1,4 +1,3 @@
-import functools
 import math
 
 import jax
@@ -8,6 +7,7 @@
 from jax.experimental import pallas as pl
 from jax.experimental.pallas import tpu as pltpu
 from jax.sharding import PartitionSpec as P
+
 
 EPS = 1e-06
 C = 384
@@ -250,12 +250,11 @@
     out_ref[...] = made[...].astype(BF16)
 
 
-def lat_sums(name, table, data):
+def lat_sums(table, data):
     count, depth = table.shape
     vmem = pl.BlockSpec(memory_space=pltpu.VMEM)
     return pl.pallas_call(
         lat_kernel,
-        name=name,
         compiler_params=grant(6),
         out_shape=jax.ShapeDtypeStruct((2 * count, LANES), BF16),
         in_specs=[vmem, vmem],
@@ -384,7 +383,9 @@
     west = [(j, i) for i, j in east]
     last = jnp.concatenate([top[:, -2:], x[:, -2:], bottom[:, -2:]], axis=0)
     first = jnp.concatenate([top[:, :2], x[:, :2], bottom[:, :2]], axis=0)
-    return lax.ppermute(last, "lon", east), lax.ppermute(first, "lon", west)
+    left = lax.ppermute(last, "lon", east)
+    right = lax.ppermute(first, "lon", west)
+    return left, right
 
 
 def per_device(grid_state, norm_gain, conv_weight, filter_weight, degree_keep):
@@ -401,9 +402,9 @@
     carried = exchange(data, "lon")
     data = lon_sums(waves, carried.reshape(LON * PAD, LANES), 1, 2.0 * math.pi / NLON)
     data = by_orders(data)
-    data = by_degrees(lat_sums("analysis", analysis, data))
+    data = by_degrees(lat_sums(analysis, data))
     data = by_degrees(filtered(degree, data, carried, filter_weight))
-    data = by_orders(lat_sums("synthesis", synthesis, data))
+    data = by_orders(lat_sums(synthesis, data))
     data = exchange(lon_sums(waves, data, 0, 1.0).reshape(LON, PAD, LANES), "lon")
     return finished(held, data)
 

time: 189 us -> 189 us (level)
  no operation moved by 1% of the time
where the time goes in v5:
time: 189 us
  blocking collectives  115 us (61%)
  starting transfers between devices  29.5 us (16%)
  waiting for transfers between devices  23.8 us (13%)
  Pallas kernels  12.9 us (7%)
  local copies, waits for them, and re-layouts  4.49 us (2%)
    all_to_all x5, blocking collectives, exchange(): lax.all_to_all(data, axis, 0, 0, tiled=True, axis_index_groups=groups)  115 us
    all_to_all x1, waiting for transfers between devices, exchange(): lax.all_to_all(data, axis, 0, 0, tiled=True, axis_index_groups=groups)  13.3 us
    all_to_all x1, starting transfers between devices, exchange(): lax.all_to_all(data, axis, 0, 0, tiled=True, axis_index_groups=groups)  11.5 us
    ppermute x1, starting transfers between devices, lon_halo(): right = lax.ppermute(first, 'lon', west)  10.9 us
    ppermute x1, waiting for transfers between devices, lon_halo(): left = lax.ppermute(last, 'lon', east)  9.09 us
    pallas_call x1, Pallas kernels, convolutions(): pl.pallas_call(conv_kernel, name='convolutions', out_shape=[jax.ShapeDtyp...  6.5 us
    ppermute x1, starting transfers between devices, lat_halo(): lax.ppermute(x[ROWS - 2:], 'lat', up)  3.92 us
  transfers between devices with their start and end apart: 5, of which 3 were waited for; matrix products, arithmetic and copies ran while one was open for 2% of the time, Pallas kernels for 1%

profile of v5, /device:TPU:1, one launch (start us, length us, event | category | flops | bytes accessed | tf_op | source)
XLA Modules:
  0.0 188.5 jit_solution(13318759331916447886)
XLA Ops:
  0.0 0.9 fusion.4
  0.9 3.9 %collective-permute-start = (f32[2,15,384]{2,1,0:T(8,128)S(1)}, f32[2,15,384]{2,1,0:T(8,128)S(1)}, u32[]{:S(2)}, u32[]{:S(2)}) collective-permute-start(f32[2,15,384]{2,1,0:T(8,128)S(1)} %get-tuple-element.22), channel_id=1, source_target_pairs={{0,48},{48,96},{96,144},{144,192},{192,240},{240,288},{288,336},{3... | collective-permute-start | bytes 138248 | tf_op jit(solution)/shard_map/ppermute | solution.py:378
  4.8 1.3 collective-permute-start.1
  6.1 1.0 fusion.3
  7.2 0.7 convert_element_type.29
  7.9 0.1 mul.55
  8.0 0.1 copy.12
  8.2 0.1 mul.59
  8.3 1.3 collective-permute-done.1.bottom_ref
  9.7 10.9 %collective-permute-start.3 = (f32[16,2,384]{2,1,0:T(2,128)S(1)}, f32[16,2,384]{2,1,0:T(2,128)S(1)}, u32[]{:S(2)}, u32[]{:S(2)}) collective-permute-start(f32[16,2,384]{2,1,0:T(2,128)S(1)} %pad_maximum_fusion.1), channel_id=1, source_target_pairs={{1,0},{2,1},{3,2},{4,3},{5,4},{6,5},{7,6},{8,7},{9,8},{10,9},{11,1... | collective-permute-start | bytes 147464 | tf_op jit(solution)/shard_map/ppermute | solution.py:387
  20.7 1.9 %collective-permute-start.2 = (f32[16,2,384]{2,1,0:T(2,128)S(1)}, f32[16,2,384]{2,1,0:T(2,128)S(1)}, u32[]{:S(2)}, u32[]{:S(2)}) collective-permute-start(f32[16,2,384]{2,1,0:T(2,128)S(1)} %pad_maximum_fusion), channel_id=1, source_target_pairs={{0,1},{1,2},{2,3},{3,4},{4,5},{5,6},{6,7},{7,8},{8,9},{9,10},{10,1... | collective-permute-start | bytes 147464 | tf_op jit(solution)/shard_map/ppermute | solution.py:386
  22.6 0.7 broadcast_multiply_fusion.keep_ref
  23.3 9.1 %collective-permute-done.2.left_ref = f32[16,2,384]{2,1,0:T(2,128)S(1)} collective-permute-done((f32[16,2,384]{2,1,0:T(2,128)S(1)}, f32[16,2,384]{2,1,0:T(2,128)S(1)}, u32[]{:S(2)}, u32[]{:S(2)}) %collective-permute-start.2) | collective-permute-done | bytes 49184 | tf_op jit(solution)/shard_map/ppermute | solution.py:386
  32.4 0.6 copy-done.7
  33.0 6.5 %convolutions.1 = (f32[12,16,384]{2,1,0:T(8,128)}, bf16[48,16,128]{2,1,0:T(8,128)(2,1)}) custom-call(s32[1]{0:T(128)} %bitcast.place_ref, f32[12,15,384]{2,1,0:T(8,128)} %x_ref.1, f32[2,15,384]{2,1,0:T(8,128)} %copy-done.4, f32[2,15,384]{2,1,0:T(8,128)} %copy-done.5, f32[16,2,384]{2,1,0:T(2,128)} %copy-done.7, f32[16,2,384]{2,1,0:T(2,128)} %copy-done.6, ...), custom_call_target="tpu_custom_call" | custom-call | flops 1358954496 | bytes 6500000 | tf_op jit(solution)/shard_map/convolutions/pallas_call | solution.py:216
  39.5 31.3 %all_to_all.30.keep_ref = bf16[48,16,128]{2,1,0:T(8,128)(2,1)S(1)} all-to-all(bf16[48,16,128]{2,1,0:T(8,128)(2,1)} %get-tuple-element.18), channel_id=1, replica_groups=mesh['lat'=16,'lon'=48] {'lon'}, dimensions={0} | all-to-all | bytes 393216 | tf_op jit(solution)/shard_map/all_to_all | solution.py:349
  70.8 0.4 fusion.2
  71.2 0.8 copy.13
  71.9 11.5 %all-to-all-start.1 = ((bf16[256,2,128]{2,1,0:T(2,128)(2,1)}), bf16[256,2,128]{2,1,0:T(2,128)(2,1)S(1)}, u32[]{:S(2)}, u32[]{:S(2)}) async-start(bf16[256,2,128]{2,1,0:T(2,128)(2,1)} %bitcast.6), calls=%async_computation.1 | async-start | bytes 262144 | tf_op jit(solution)/shard_map/all_to_all | solution.py:349
  83.5 0.7 dynamic-slice_bitcast_fusion.coeff_ref.start_ref
  84.2 1.8 legendre.1
  86.0 13.3 %all-to-all-done.1 = bf16[256,2,128]{2,1,0:T(2,128)(2,1)S(1)} async-done(((bf16[256,2,128]{2,1,0:T(2,128)(2,1)}), bf16[256,2,128]{2,1,0:T(2,128)(2,1)S(1)}, u32[]{:S(2)}, u32[]{:S(2)}) %all-to-all-start.1) | async-done | bytes 131104 | tf_op jit(solution)/shard_map/all_to_all | solution.py:349
  99.3 0.2 shard_map.82
  99.5 16.0 %all_to_all.31 = bf16[48,8,128]{2,1,0:T(8,128)(2,1)} all-to-all(bf16[48,8,128]{2,1,0:T(8,128)(2,1)S(1)} %bitcast.28), channel_id=1, replica_groups={{0,2,4,48,50,52,96,98,100,144,146,148,192,194,196,240,242,244,288,290,2..., dimensions={0} | all-to-all | bytes 196608 | tf_op jit(solution)/shard_map/all_to_all | solution.py:349
  115.6 3.3 %filter.1 = bf16[384,128]{1,0:T(8,128)(2,1)} custom-call(s32[1]{0:T(128)} %bitcast.3.first_ref, bf16[384,128]{1,0:T(8,128)(2,1)} %bitcast.32, bf16[48,16,128]{2,1,0:T(8,128)(2,1)} %copy-done.3, bf16[12,384,384]{2,1,0:T(8,128)(2,1)} %weight_ref.3), custom_call_target="tpu_custom_call" | custom-call | flops 301989888 | bytes 1700000 | tf_op jit(solution)/shard_map/filter/pallas_call | solution.py:307
  118.9 13.4 %all_to_all.32 = bf16[48,8,128]{2,1,0:T(8,128)(2,1)S(1)} all-to-all(bf16[48,8,128]{2,1,0:T(8,128)(2,1)} %bitcast.33), channel_id=1, replica_groups={{0,2,4,48,50,52,96,98,100,144,146,148,192,194,196,240,242,244,288,290,2..., dimensions={0} | all-to-all | bytes 196608 | tf_op jit(solution)/shard_map/all_to_all | solution.py:349
  132.2 0.2 shard_map.83
  132.5 30.8 %all_to_all.33 = bf16[256,2,128]{2,1,0:T(2,128)(2,1)S(1)} all-to-all(bf16[256,2,128]{2,1,0:T(2,128)(2,1)S(1)} %bitcast.26), channel_id=1, replica_groups={{0,1,6,7,12,13,18,19,24,25,30,31,36,37,42,43,48,49,54,55,60,61,66,67,72..., dimensions={0} | all-to-all | bytes 262144 | tf_op jit(solution)/shard_map/all_to_all | solution.py:349
  163.3 0.3 fusion
  163.6 0.2 copy.14
  163.7 24.0 %all_to_all.34.in_ref = bf16[48,16,128]{2,1,0:T(8,128)(2,1)S(1)} all-to-all(bf16[48,16,128]{2,1,0:T(8,128)(2,1)S(1)} %bitcast.30), channel_id=1, replica_groups=mesh['lat'=16,'lon'=48] {'lon'}, dimensions={0} | all-to-all | bytes 393216 | tf_op jit(solution)/shard_map/all_to_all | solution.py:349
  187.7 0.8 finish.1
  (24 shorter events, 0.2 us)
Async XLA Ops:
  0.0 70.8 %copy-start.2 = (bf16[512,768]{1,0:T(8,128)(2,1)S(1)}, bf16[512,768]{1,0:T(8,128)(2,1)}, u32[]{:S(2)}) copy-start(bf16[512,768]{1,0:T(8,128)(2,1)} %constant.78.clone) | copy-start | bytes 2359300
  0.0 84.2 %copy-start.1 = (f32[2,256]{1,0:T(2,128)S(1)}, f32[2,256]{1,0:T(2,128)}, u32[]{:S(2)}) copy-start(f32[2,256]{1,0:T(2,128)} %constant.80.clone.rows_ref) | copy-start | bytes 6148
  0.9 7.4 %collective-permute-start = (f32[2,15,384]{2,1,0:T(8,128)S(1)}, f32[2,15,384]{2,1,0:T(8,128)S(1)}, u32[]{:S(2)}, u32[]{:S(2)}) collective-permute-start(f32[2,15,384]{2,1,0:T(8,128)S(1)} %get-tuple-element.22), channel_id=1, source_target_pairs={{0,48},{48,96},{96,144},{144,192},{192,240},{240,288},{288,336},{3... | collective-permute-start | bytes 138248 | tf_op jit(solution)/shard_map/ppermute | solution.py:378
  4.8 4.8 %collective-permute-start.1 = (f32[2,15,384]{2,1,0:T(8,128)S(1)}, f32[2,15,384]{2,1,0:T(8,128)S(1)}, u32[]{:S(2)}, u32[]{:S(2)}) collective-permute-start(f32[2,15,384]{2,1,0:T(8,128)S(1)} %get-tuple-element.21), channel_id=1, source_target_pairs={{48,0},{96,48},{144,96},{192,144},{240,192},{288,240},{336,288},{3... | collective-permute-start | bytes 138248 | tf_op jit(solution)/shard_map/ppermute | solution.py:378
  8.3 24.0 %copy-start.4 = (f32[2,15,384]{2,1,0:T(8,128)}, f32[2,15,384]{2,1,0:T(8,128)S(1)}, u32[]{:S(2)}) copy-start(f32[2,15,384]{2,1,0:T(8,128)S(1)} %collective-permute-done.top_ref) | copy-start | bytes 138244
  9.7 22.7 %copy-start.5 = (f32[2,15,384]{2,1,0:T(8,128)}, f32[2,15,384]{2,1,0:T(8,128)S(1)}, u32[]{:S(2)}) copy-start(f32[2,15,384]{2,1,0:T(8,128)S(1)} %collective-permute-done.1.bottom_ref) | copy-start | bytes 138244
  9.7 13.5 %collective-permute-start.3 = (f32[16,2,384]{2,1,0:T(2,128)S(1)}, f32[16,2,384]{2,1,0:T(2,128)S(1)}, u32[]{:S(2)}, u32[]{:S(2)}) collective-permute-start(f32[16,2,384]{2,1,0:T(2,128)S(1)} %pad_maximum_fusion.1), channel_id=1, source_target_pairs={{1,0},{2,1},{3,2},{4,3},{5,4},{6,5},{7,6},{8,7},{9,8},{10,9},{11,1... | collective-permute-start | bytes 147464 | tf_op jit(solution)/shard_map/ppermute | solution.py:387
  20.7 11.7 %collective-permute-start.2 = (f32[16,2,384]{2,1,0:T(2,128)S(1)}, f32[16,2,384]{2,1,0:T(2,128)S(1)}, u32[]{:S(2)}, u32[]{:S(2)}) collective-permute-start(f32[16,2,384]{2,1,0:T(2,128)S(1)} %pad_maximum_fusion), channel_id=1, source_target_pairs={{0,1},{1,2},{2,3},{3,4},{4,5},{5,6},{6,7},{7,8},{8,9},{9,10},{10,1... | collective-permute-start | bytes 147464 | tf_op jit(solution)/shard_map/ppermute | solution.py:386
  23.3 9.1 %copy-start.6 = (f32[16,2,384]{2,1,0:T(2,128)}, f32[16,2,384]{2,1,0:T(2,128)S(1)}, u32[]{:S(2)}) copy-start(f32[16,2,384]{2,1,0:T(2,128)S(1)} %collective-permute-done.3.right_ref) | copy-start | bytes 147460
  32.4 0.6 copy-start.7
  39.5 148.2 %copy-start = (f32[12,16,384]{2,1,0:T(8,128)S(1)}, f32[12,16,384]{2,1,0:T(8,128)}, u32[]{:S(2)}) copy-start(f32[12,16,384]{2,1,0:T(8,128)} %get-tuple-element.14.held_ref) | copy-start | bytes 884740
  70.8 44.8 %copy-start.3 = (bf16[48,16,128]{2,1,0:T(8,128)(2,1)}, bf16[48,16,128]{2,1,0:T(8,128)(2,1)S(1)}, u32[]{:S(2)}) copy-start(bf16[48,16,128]{2,1,0:T(8,128)(2,1)S(1)} %all_to_all.30.keep_ref) | copy-start | bytes 589828
  71.9 27.4 %all-to-all-start.1 = ((bf16[256,2,128]{2,1,0:T(2,128)(2,1)}), bf16[256,2,128]{2,1,0:T(2,128)(2,1)S(1)}, u32[]{:S(2)}, u32[]{:S(2)}) async-start(bf16[256,2,128]{2,1,0:T(2,128)(2,1)} %bitcast.6), calls=%async_computation.1 | async-start | bytes 262144 | tf_op jit(solution)/shard_map/all_to_all | solution.py:349
